TPU v7x, 512 devices: a whole 4x8x8 slice. The times are simulated.
512 devices in a mesh: grid: 64 (over z, x, core), col: 8 (over y).
Axes of the slice: x: 4, y: 8, z: 8, core: 2. Of those that a mesh axis runs over, the one named last changes fastest.
Arguments:
- density: bfloat16 [16384, 16384], P('grid', 'col'), may hold values from -0.125 to 0.125
- centres: float32 [3, 16384], replicated, may hold values from -0.4 to 0.4
- exponents: float32 [16384], replicated, may hold values from 2 to 16
- coords: float32 [256, 3, 256], P('grid'), may hold values from -0.4 to 0.4
- weights: float32 [256, 256], P('grid'), may hold values from 0.078125 to 0.78125
- core_density: float32 [256, 256], P('grid'), may hold values from 0.3 to 3
- counts: int32 [256], P('grid'), may hold values from 1 to 256, 16384 in all
- blocks: int32 [256, 8], replicated, may hold values from 0 to 127, as said below
Outputs:
- potential_matrix_xc: float32 [16384, 16384], P('grid', 'col')
- orbital_charge_samples: float32 [256, 256], P('grid')
- xc_batch_amounts: float32 [256], P('grid')
Inputs may be any that keep to these rules, and one draw needn't show every extreme that they name: Entry c of a batch's row names a block in the c-th of 8 equal runs of 16 blocks; for one grid index's 4 batches the values // 2 in one column c are distinct. The points in use are the first counts[b] slots.
All inputs are finite; a program needn't handle non-finite values. No bound on the sum of `counts` on one device may be relied on, other than what follows from the above.
Results may differ from a plain program's by a relative error of at most 0.0028.
Values may be sent and summed in bfloat16 or wider, within the bound.
No kernel may reach another device: no remote copies, remote signals or barrier semaphores. Data moves between devices by JAX's collectives and lax.ppermute only.
A program may use at most 64 MiB of HBM per device.

v0:
```python
from functools import partial
import math

import jax
import jax.numpy as jnp
from jax import lax
from jax.sharding import PartitionSpec as P

BLK = 128
NB = 4
SUB = 128


kappa_pbe = 0.804
mu_coef = 0.2195
slater = -0.7385587663820224
grad_scale = 4.0 * (3.0 * math.pi**2) ** (2.0 / 3.0)
soft_square = 0.25


def sent_to_all(array, axis):
    copies = jnp.broadcast_to(array, (lax.axis_size(axis), *array.shape))
    return lax.all_to_all(copies, axis, split_axis=0, concat_axis=0, tiled=True)


def taken_together(array, axis):
    everything = sent_to_all(array, axis)
    return jnp.sum(everything, axis=0)


def pbe_energy(total, grad_square):
    regular = 0.5 * (total + jnp.sqrt(total * total + soft_square))
    scaled = grad_scale * jnp.power(regular, 8.0 / 3.0)
    enhance = (
        1.0
        + kappa_pbe
        - kappa_pbe * kappa_pbe * scaled / (kappa_pbe * scaled + mu_coef * grad_square)
    )
    return slater * jnp.power(regular, 4.0 / 3.0) * enhance


def xc_kernel(total, grad_square):
    total_functional_sum, pullback = jax.vjp(pbe_energy, total, grad_square)
    charge_derivative, deriv_sigma = pullback(jnp.ones_like(total_functional_sum))
    return (total_functional_sum, charge_derivative, deriv_sigma)


def basis(points, centre_rows, rate_rows):
    offset = points[:, :, None] - centre_rows[:, None, :]
    distance = jnp.sum(offset * offset, axis=0)
    value_entries = jnp.exp(-rate_rows[None, :] * distance)
    slopes = -2.0 * rate_rows[None, None, :] * offset * value_entries[None]
    return (value_entries, slopes)


def first_pass(batch_points, centre_rows, rate_rows, tile_panel, column, block_step, buffer):
    first_row = block_step * SUB
    points = lax.dynamic_slice_in_dim(batch_points, first_row, SUB, 1)
    value_entries, slopes = basis(points, centre_rows, rate_rows)
    values_low = value_entries.astype(jnp.bfloat16)
    own_low = lax.dynamic_slice_in_dim(values_low, column * BLK, BLK, 1)
    own_values = lax.dynamic_slice_in_dim(value_entries, column * BLK, BLK, 1)
    own_slopes = lax.dynamic_slice_in_dim(slopes, column * BLK, BLK, 2)
    right_sum = jnp.dot(values_low, tile_panel, preferred_element_type=jnp.float32)
    left_sum = lax.dot_general(
        own_low, tile_panel, (((1,), (1,)), ((), ())), preferred_element_type=jnp.float32
    )
    density_part = jnp.sum(own_values * right_sum, axis=1)
    gradient_part = jnp.sum(slopes * left_sum[None], axis=2) + jnp.sum(
        own_slopes * right_sum[None], axis=2
    )
    sub_piece = jnp.concatenate([density_part[None], gradient_part], axis=0)
    return lax.dynamic_update_slice_in_dim(buffer, sub_piece, first_row, 1)


def second_pass(
    batch_points, centre_rows, rate_rows, fweight, hweight, column, block_step, total_tile
):
    first_row = block_step * SUB
    points = lax.dynamic_slice_in_dim(batch_points, first_row, SUB, 1)
    fweight_sub = lax.dynamic_slice_in_dim(fweight, first_row, SUB, 0)
    hweight_sub = lax.dynamic_slice_in_dim(hweight, first_row, SUB, 1)
    value_entries, slopes = basis(points, centre_rows, rate_rows)
    values_low = value_entries.astype(jnp.bfloat16)
    across = jnp.sum(hweight_sub[:, :, None] * slopes, axis=0)
    along = fweight_sub[:, None] * lax.dynamic_slice_in_dim(
        value_entries, column * BLK, BLK, 1
    ) + lax.dynamic_slice_in_dim(across, column * BLK, BLK, 1)
    own_low = lax.dynamic_slice_in_dim(values_low, column * BLK, BLK, 1)
    left_side = jnp.concatenate([values_low, across.astype(jnp.bfloat16)], axis=0)
    right_side = jnp.concatenate([along.astype(jnp.bfloat16), own_low], axis=0)
    return total_tile + lax.dot_general(
        left_side, right_side, (((0,), (0,)), ((), ())), preferred_element_type=jnp.float32
    )


def kernel_on(summed, live_mask, point_weights, core_density):
    valence = live_mask * summed[:, 0]
    gradient = live_mask[:, None] * summed[:, 1:]
    grad_square = jnp.sum(gradient * gradient, axis=1)
    total_functional_sum, charge_derivative, deriv_sigma = xc_kernel(
        valence + core_density, grad_square
    )
    point_scale = point_weights * live_mask
    fweight = point_scale * charge_derivative
    hweight = (2.0 * point_scale * deriv_sigma)[:, None] * gradient
    return jnp.concatenate(
        [
            fweight[:, None],
            hweight,
            valence[:, None],
            (point_scale * total_functional_sum)[:, None],
        ],
        axis=1,
    )


def local(density, centres, exponents, coords, weights, core_density, counts, blocks):
    grid_point_count = lax.axis_size("grid")
    column_count = lax.axis_size("col")
    grid_index = lax.axis_index("grid")
    column = lax.axis_index("col")
    row_blocks = density.shape[0] // BLK
    col_blocks = density.shape[1] // BLK
    owner_groups = grid_point_count // column_count
    span_width = column_count * BLK
    points_len = coords.shape[2]
    offsets = jnp.arange(BLK, dtype=jnp.int32)
    block_table = blocks.reshape(grid_point_count, NB, column_count)
    held_rows = lax.dynamic_index_in_dim(block_table, grid_index, 0, keepdims=False)
    asked_rows = lax.dynamic_index_in_dim(
        block_table, grid_index // owner_groups, 2, keepdims=False
    )
    asked_cols = lax.dynamic_index_in_dim(block_table, column, 2, keepdims=False)
    matched = asked_rows // row_blocks == grid_index
    local_tile = asked_rows % row_blocks * col_blocks + asked_cols - column * col_blocks
    tile_slot = jnp.sum(jnp.where(matched, local_tile, 0), axis=1)
    has_tile = jnp.any(matched, axis=1)
    tile_ids = jnp.arange(row_blocks * col_blocks, dtype=jnp.int32)
    onehot = jnp.where(
        has_tile[:, None] & (tile_slot[:, None] == tile_ids[None, :]), 1.0, 0.0
    ).astype(jnp.float32)
    local_tiles = (
        density.reshape(row_blocks, BLK, col_blocks, BLK)
        .transpose(0, 2, 1, 3)
        .reshape(row_blocks * col_blocks, BLK * BLK)
    )
    outgoing = jnp.where(
        has_tile[:, None], jnp.take(local_tiles, tile_slot, axis=0), jnp.zeros((), jnp.bfloat16)
    )
    incoming = lax.all_to_all(outgoing, "grid", split_axis=0, concat_axis=0, tiled=True)
    holder_ranks = (held_rows // row_blocks).reshape(-1)
    fetched = jnp.take(incoming, holder_ranks, axis=0).reshape(NB, span_width, BLK)
    live_mask = (jnp.arange(points_len, dtype=jnp.int32)[None, :] < counts[:, None]).astype(
        jnp.float32
    )
    centre_list = []
    rate_list = []
    accumulated_totals = []
    for batch_id in range(NB):
        func_index = (held_rows[batch_id][:, None] * BLK + offsets[None, :]).reshape(-1)
        centre_rows = jnp.take(centres, func_index, axis=1)
        rate_rows = jnp.take(exponents, func_index)
        centre_list.append(centre_rows)
        rate_list.append(rate_rows)
        completed_steps = (counts[batch_id] + SUB - 1) // SUB
        step_function = partial(
            first_pass, coords[batch_id], centre_rows, rate_rows, fetched[batch_id], column
        )
        accumulated_totals.append(
            lax.fori_loop(
                0, completed_steps, step_function, jnp.zeros((4, points_len), jnp.float32)
            )
        )
    stacked = jnp.stack(accumulated_totals, axis=0)
    summed = taken_together(stacked, "col")
    results = kernel_on(summed, live_mask, weights, core_density)
    tile_list = []
    for batch_id in range(NB):
        completed_steps = (counts[batch_id] + SUB - 1) // SUB
        step_function = partial(
            second_pass,
            coords[batch_id],
            centre_list[batch_id],
            rate_list[batch_id],
            results[batch_id, 0],
            results[batch_id, 1:4],
            column,
        )
        block_result_value = lax.fori_loop(
            0, completed_steps, step_function, jnp.zeros((span_width, BLK), jnp.float32)
        )
        tile_list.append(block_result_value.reshape(column_count, BLK * BLK))
    sending = (
        jnp.zeros((grid_point_count, BLK * BLK), jnp.float32)
        .at[holder_ranks]
        .set(jnp.concatenate(tile_list, axis=0))
    )
    arrived = lax.all_to_all(sending, "grid", split_axis=0, concat_axis=0, tiled=True)
    gathered = lax.dot_general(
        onehot,
        arrived,
        (((0,), (0,)), ((), ())),
        precision=lax.Precision.HIGHEST,
        preferred_element_type=jnp.float32,
    )
    potential_matrix_xc = (
        gathered.reshape(row_blocks, col_blocks, BLK, BLK)
        .transpose(0, 2, 1, 3)
        .reshape(row_blocks * BLK, col_blocks * BLK)
    )
    orbital_charge_samples = results[:, 4]
    xc_batch_amounts = jnp.sum(results[:, 5], axis=1)
    return (potential_matrix_xc, orbital_charge_samples, xc_batch_amounts)


def solution(mesh):
    return jax.shard_map(
        local,
        mesh=mesh,
        in_specs=(
            P("grid", "col"),
            P(),
            P(),
            P("grid", None, None),
            P("grid", None),
            P("grid", None),
            P("grid"),
            P(),
        ),
        out_specs=(P("grid", "col"), P("grid", None), P("grid")),
        check_vma=False,
    )
```

profile of v0, /device:TPU:1, one launch (start us, length us, event | category | flops | bytes accessed | tf_op | source)
XLA Modules:
  0.0 287.6 jit_solution(6439348604067840900)
XLA Ops:
  0.7 0.8 copy.199
  2.0 1.5 copy.234
  3.8 0.7 copy.255
  4.5 3.2 %gather_fusion = bf16[64,16384]{1,0:T(8,128)(2,1)} fusion(bf16[32,16384]{1,0:T(8,128)(2,1)S(1)} %bitcast.257, s32[1024]{0:T(1024)S(1)} %pad_clamp_fusion.1), kind=kCustom, calls=%fused_computation.8 | custom fusion | bytes 4194560 | tf_op jit(solution)/shard_map/jit(_take)/gather | solution.py:149
  7.7 1.9 fusion.74
  10.1 2.9 %reduce = bf16[64,16384]{1,0:T(8,128)(2,1)} reduce(bf16[64,1,16384]{2,0,1:T(8,128)(2,1)S(1)} %fusion.74, bf16[]{:T(256)} %broadcast.707), dimensions={1}, to_apply=%copy.205.reduce_sub_computation | reduce | bytes 4194306 | tf_op jit(solution)/shard_map/jit(_where)/select_n | solution.py:148
  13.0 4.5 %reshape.737 = bf16[64,2,8192]{2,1,0:T(2,128)(2,1)} reshape(bf16[64,16384]{1,0:T(8,128)(2,1)} %reduce) | data formatting | bytes 4194304
  17.5 15.0 %all-to-all-start = ((bf16[64,2,8192]{2,1,0:T(2,128)(2,1)}), bf16[64,2,8192]{2,1,0:T(2,128)(2,1)S(1)}, u32[]{:S(2)}, u32[]{:S(2)}) async-start(bf16[64,2,8192]{2,1,0:T(2,128)(2,1)} %reshape.737), calls=%async_computation | async-start | bytes 4194304 | tf_op jit(solution)/shard_map/all_to_all | solution.py:151
  32.7 0.6 fusion.137
  34.6 5.1 %copy.203 = f32[3,16384]{0,1:T(8,128)} copy(f32[3,16384]{1,0:T(4,128)S(1)} %copy-done.10) | data formatting | bytes 393216 | tf_op args[1]
  39.8 7.4 %gather_fusion.3 = f32[1024,3]{1,0:T(8,128)} fusion(f32[3,16384]{0,1:T(8,128)} %copy.203, s32[1024]{0:T(1024)S(1)} %get-tuple-element.1672), kind=kCustom, calls=%fused_computation.clone | custom fusion | bytes 28672 | tf_op jit(solution)/shard_map/jit(_take)/gather | solution.py:162
  47.1 6.1 %gather_fusion.2 = f32[1024]{0:T(1024)S(1)} fusion(f32[16384]{0:T(1024)S(1)} %copy-done, s32[1024]{0:T(1024)S(1)} %get-tuple-element.1672), kind=kCustom, calls=%fused_computation.1.clone | custom fusion | bytes 12288 | tf_op jit(solution)/shard_map/jit(_take)/gather | solution.py:163
  53.3 7.4 %gather_fusion.5 = f32[1024,3]{1,0:T(8,128)} fusion(f32[3,16384]{0,1:T(8,128)} %copy.203, s32[1024]{0:T(1024)S(1)} %get-tuple-element.1671), kind=kCustom, calls=%fused_computation.2.clone | custom fusion | bytes 28672 | tf_op jit(solution)/shard_map/jit(_take)/gather | solution.py:162
  60.6 6.1 %gather_fusion.4 = f32[1024]{0:T(1024)S(1)} fusion(f32[16384]{0:T(1024)S(1)} %copy-done, s32[1024]{0:T(1024)S(1)} %get-tuple-element.1671), kind=kCustom, calls=%fused_computation.5.clone | custom fusion | bytes 12288 | tf_op jit(solution)/shard_map/jit(_take)/gather | solution.py:163
  67.5 7.4 %gather_fusion.7 = f32[1024,3]{1,0:T(8,128)} fusion(f32[3,16384]{0,1:T(8,128)} %copy.203, s32[1024]{0:T(1024)S(1)} %get-tuple-element.1670), kind=kCustom, calls=%fused_computation.3.clone | custom fusion | bytes 28672 | tf_op jit(solution)/shard_map/jit(_take)/gather | solution.py:162
  74.9 6.1 %gather_fusion.6 = f32[1024]{0:T(1024)S(1)} fusion(f32[16384]{0:T(1024)S(1)} %copy-done, s32[1024]{0:T(1024)S(1)} %get-tuple-element.1670), kind=kCustom, calls=%fused_computation.6.clone | custom fusion | bytes 12288 | tf_op jit(solution)/shard_map/jit(_take)/gather | solution.py:163
  81.7 6.2 %gather_fusion.9 = f32[1024,3]{1,0:T(8,128)S(1)} fusion(f32[3,16384]{0,1:T(8,128)} %copy.203, s32[1024]{0:T(1024)S(1)} %get-tuple-element.1669), kind=kCustom, calls=%fused_computation.4.clone | custom fusion | bytes 28672 | tf_op jit(solution)/shard_map/jit(_take)/gather | solution.py:162
  87.9 6.2 %gather_fusion.8 = f32[1024]{0:T(1024)S(1)} fusion(f32[16384]{0:T(1024)S(1)} %copy-done, s32[1024]{0:T(1024)S(1)} %get-tuple-element.1669), kind=kCustom, calls=%fused_computation.7.clone | custom fusion | bytes 12288 | tf_op jit(solution)/shard_map/jit(_take)/gather | solution.py:163
  94.2 1.2 select_bitcast_fusion.3
  95.6 1.3 select_bitcast_fusion.2
  97.1 1.3 select_bitcast_fusion.1
  100.0 6.8 %reshape.738 = bf16[64,1,16384]{2,1,0:T(2,128)(2,1)} reshape(bf16[64,2,8192]{2,1,0:T(2,128)(2,1)S(1)} %all-to-all-done) | data formatting | bytes 4194304
  106.7 4.5 %copy.254 = bf16[64,1,16384]{2,0,1:T(8,128)(2,1)S(1)} copy(bf16[64,1,16384]{2,1,0:T(2,128)(2,1)} %reshape.738) | data formatting | bytes 4194304
  111.2 1.2 gather_fusion.1
  112.6 0.9 fusion.134
  113.6 3.1 %while.96 = (s32[]{:T(128)}, f32[4,256]{1,0:T(4,128)S(1)}, s32[]{:T(128)}, f32[1,1024]{1,0:T(1,128)S(1)}, f32[3,256]{1,0:T(4,128)S(1)}, /*index=5*/f32[3,1024]{1...) while((s32[]{:T(128)}, f32[4,256]{1,0:T(4,128)S(1)}, ...), condition=%wide.region_7.10_spmd, body=%wide.region_2.9_spmd.sunk | while | flops 70517760 | bytes 10578679 | solution.py:171
  116.7 1.1 squeeze.83
  117.8 6.2 %while.97 = (s32[]{:T(128)}, f32[4,256]{1,0:T(4,128)S(1)}, s32[]{:T(128)}, f32[1,1024]{1,0:T(1,128)S(1)}, f32[3,256]{1,0:T(4,128)S(1)}, /*index=5*/f32[3,1024]{1...) while((s32[]{:T(128)}, f32[4,256]{1,0:T(4,128)S(1)}, ...), condition=%wide.region_13.16_spmd, body=%wide.region_8.15_spmd.sunk | while | flops 70517760 | bytes 10578679 | solution.py:171
  124.1 1.1 squeeze.85
  125.2 3.3 %while.98 = (s32[]{:T(128)}, f32[4,256]{1,0:T(4,128)S(1)}, s32[]{:T(128)}, f32[1,1024]{1,0:T(1,128)S(1)}, f32[3,256]{1,0:T(4,128)S(1)}, /*index=5*/f32[3,1024]{1...) while((s32[]{:T(128)}, f32[4,256]{1,0:T(4,128)S(1)}, ...), condition=%wide.region_19.22_spmd, body=%wide.region_14.21_spmd.sunk | while | flops 70517760 | bytes 10578679 | solution.py:171
  128.5 1.1 squeeze.87
  129.6 0.6 broadcast.548.clone
  130.2 3.7 %while.99 = (s32[]{:T(128)}, f32[4,256]{1,0:T(4,128)}, s32[]{:T(128)}, f32[1,1024]{1,0:T(1,128)S(1)}, f32[3,256]{1,0:T(4,128)S(1)}, /*index=5*/f32[3,1024]{1,0:T...) while((s32[]{:T(128)}, f32[4,256]{1,0:T(4,128)}, ...), condition=%wide.region_25.28_spmd, body=%wide.region_20.27_spmd.sunk | while | flops 70517760 | bytes 10578167 | solution.py:171
  133.8 0.7 pad_maximum_fusion
  134.5 0.7 broadcast_in_dim.120
  135.2 6.8 %all-to-all-start.1 = ((f32[8,4,4,256]{3,2,1,0:T(4,128)}), f32[8,4,4,256]{3,2,1,0:T(4,128)S(1)}, u32[]{:S(2)}, u32[]{:S(2)}) async-start(f32[8,4,4,256]{3,2,1,0:T(4,128)} %broadcast_in_dim.120), calls=%async_computation.1 | async-start | bytes 262144 | tf_op jit(solution)/shard_map/all_to_all | solution.py:23
  142.1 7.9 %all-to-all-done.1 = f32[8,4,4,256]{3,2,1,0:T(4,128)S(1)} async-done(((f32[8,4,4,256]{3,2,1,0:T(4,128)}), f32[8,4,4,256]{3,2,1,0:T(4,128)S(1)}, u32[]{:S(2)}, u32[]{:S(2)}) %all-to-all-start.1) | async-done | bytes 131104 | tf_op jit(solution)/shard_map/all_to_all | solution.py:23
  150.1 0.7 multiply_reduce_fusion.13
  151.4 1.3 while.100
  152.9 2.7 while.101
  155.7 1.3 while.102
  157.2 1.3 while.103
  158.7 4.2 %scatter_custom_fusion = f32[64,16384]{1,0:T(8,128)} fusion(s32[32]{0:T(128)} %copy-done.20, f32[8,16384]{1,0:T(8,128)S(1)} %reshape.619, f32[]{:T(128)} %constant.480, f32[8,16384]{1,0:T(8,128)S(1)} %reshape.618, f32[8,16384]{1,0:T(8,128)S(1)} %reshape.617, f32[8,16384]{1,0:T(8,128)S(1)} %reshape.616, f32[]{:T(128)} %constant.438.clone.1), kind=kCustom, calls=%fused_computation.152 | custom fusion | flops 1572864 | bytes 6292480 | tf_op jit(solution)/shard_map/scatter | solution.py:197
  162.8 6.0 %all_to_all.20 = f32[64,1,16384]{2,1,0:T(1,128)} reshape(f32[64,16384]{1,0:T(8,128)} %scatter_custom_fusion) | data formatting | bytes 8388608 | tf_op jit(solution)/shard_map/all_to_all | solution.py:199
  168.8 14.9 %all-to-all-start.2 = ((f32[64,1,16384]{2,1,0:T(1,128)}), f32[64,1,16384]{2,1,0:T(1,128)}, u32[]{:S(2)}, u32[]{:S(2)}) async-start(f32[64,1,16384]{2,1,0:T(1,128)} %all_to_all.20), calls=%async_computation.2 | async-start | bytes 8388608 | tf_op jit(solution)/shard_map/all_to_all | solution.py:199
  183.7 94.7 %all-to-all-done.2 = f32[64,1,16384]{2,1,0:T(1,128)} async-done(((f32[64,1,16384]{2,1,0:T(1,128)}), f32[64,1,16384]{2,1,0:T(1,128)}, u32[]{:S(2)}, u32[]{:S(2)}) %all-to-all-start.2) | async-done | bytes 4194336 | tf_op jit(solution)/shard_map/all_to_all | solution.py:199
  278.4 7.0 %fusion.64 = f32[2,16,128,128]{3,1,2,0:T(8,128)S(1)} fusion(s32[2,16]{1,0:T(2,128)S(1)} %multiply_add_fusion.1, s32[64]{0:T(128)S(1)} %copy-done.19, pred[64]{0:T(512)(128)(4,1)S(1)} %copy-done.17, f32[64,1,16384]{2,1,0:T(1,128)} %all-to-all-done.2), kind=kOutput, calls=%fused_computation.148 | convolution fusion | flops 402659328 | bytes 6291904 | tf_op jit(solution)/shard_map/dot_general | solution.py:200
  285.4 2.2 copy.253
  (217 shorter events, 27.0 us)
Async XLA Ops:
  0.6 46.5 %copy-start = (f32[16384]{0:T(1024)S(1)}, f32[16384]{0:T(1024)}, u32[]{:S(2)}) copy-start(f32[16384]{0:T(1024)} %param.30) | copy-start | bytes 196612
  1.8 5.8 %copy-start.16 = (pred[64]{0:T(512)(128)(4,1)}, pred[64]{0:T(512)(128)(4,1)S(1)}, u32[]{:S(2)}) copy-start(pred[64]{0:T(512)(128)(4,1)S(1)} %get-tuple-element.1613) | copy-start | bytes 196
  2.0 1.8 copy-start.18
  17.5 15.2 %copy-start.11 = (s32[4]{0:T(128)S(1)}, s32[4]{0:T(128)}, u32[]{:S(2)}) copy-start(s32[4]{0:T(128)} %param.34) | copy-start | bytes 52
  17.5 17.1 %copy-start.10 = (f32[3,16384]{1,0:T(4,128)S(1)}, f32[3,16384]{1,0:T(4,128)}, u32[]{:S(2)}) copy-start(f32[3,16384]{1,0:T(4,128)} %param.29) | copy-start | bytes 589828
  17.5 82.4 %all-to-all-start = ((bf16[64,2,8192]{2,1,0:T(2,128)(2,1)}), bf16[64,2,8192]{2,1,0:T(2,128)(2,1)S(1)}, u32[]{:S(2)}, u32[]{:S(2)}) async-start(bf16[64,2,8192]{2,1,0:T(2,128)(2,1)} %reshape.737), calls=%async_computation | async-start | bytes 4194304 | tf_op jit(solution)/shard_map/all_to_all | solution.py:151
  97.1 2.8 copy-start.15
  99.0 0.6 copy-start.20
  114.3 0.7 copy-start.2
  115.2 1.0 copy-start.3
  118.5 0.7 copy-start.4
  119.4 1.0 copy-start.5
  121.6 0.7 copy-start.4
  122.5 1.0 copy-start.5
  126.1 0.7 copy-start.6
  127.0 1.0 copy-start.7
  130.2 19.9 %copy-start.12 = (f32[4,256]{1,0:T(4,128)S(1)}, f32[4,256]{1,0:T(4,128)}, u32[]{:S(2)}) copy-start(f32[4,256]{1,0:T(4,128)} %param.32) | copy-start | bytes 12292
  130.2 19.9 %copy-start.13 = (f32[4,256]{1,0:T(4,128)S(1)}, f32[4,256]{1,0:T(4,128)}, u32[]{:S(2)}) copy-start(f32[4,256]{1,0:T(4,128)} %param.33) | copy-start | bytes 12292
  130.8 0.7 copy-start.8
  131.7 1.0 copy-start.9
  135.2 14.8 %all-to-all-start.1 = ((f32[8,4,4,256]{3,2,1,0:T(4,128)}), f32[8,4,4,256]{3,2,1,0:T(4,128)S(1)}, u32[]{:S(2)}, u32[]{:S(2)}) async-start(f32[8,4,4,256]{3,2,1,0:T(4,128)} %broadcast_in_dim.120), calls=%async_computation.1 | async-start | bytes 262144 | tf_op jit(solution)/shard_map/all_to_all | solution.py:23
  150.8 0.6 copy-start.14
  168.8 109.6 %copy-start.17 = (pred[64]{0:T(512)(128)(4,1)S(1)}, pred[64]{0:T(512)(128)(4,1)}, u32[]{:S(2)}) copy-start(pred[64]{0:T(512)(128)(4,1)} %copy-done.16) | copy-start | bytes 196
  168.8 109.6 %copy-start.19 = (s32[64]{0:T(128)S(1)}, s32[64]{0:T(128)}, u32[]{:S(2)}) copy-start(s32[64]{0:T(128)} %copy-done.18) | copy-start | bytes 772
  168.8 109.6 %all-to-all-start.2 = ((f32[64,1,16384]{2,1,0:T(1,128)}), f32[64,1,16384]{2,1,0:T(1,128)}, u32[]{:S(2)}, u32[]{:S(2)}) async-start(f32[64,1,16384]{2,1,0:T(1,128)} %all_to_all.20), calls=%async_computation.2 | async-start | bytes 8388608 | tf_op jit(solution)/shard_map/all_to_all | solution.py:199
  285.4 2.2 copy-start.1
where the time goes:
time: 293 us; the launch traced here: 288 us
  local copies, waits for them, and re-layouts  107 us (37%)
  waiting for transfers between devices  103 us (35%)
  starting transfers between devices  36.7 us (13%)
  other arithmetic  25.2 us (9%)
  matrix products  11.5 us (4%)
  between operations  3.81 us (1%)
    all_to_all x1, waiting for transfers between devices, local(): lax.all_to_all(sending, 'grid', split_axis=0, concat_axis=0, tiled=True)  94.7 us
    gather x4, local copies, waits for them, and re-layouts, local(): centre_rows = jnp.take(centres, func_index, axis=1)  28.3 us
    unnamed x34, local copies, waits for them, and re-layouts  27 us
    gather x4, local copies, waits for them, and re-layouts, local(): rate_rows = jnp.take(exponents, func_index)  24.6 us
    all_to_all x1, starting transfers between devices, local(): lax.all_to_all(outgoing, 'grid', split_axis=0, concat_axis=0, tiled=True)  15 us
    all_to_all x1, starting transfers between devices, local(): lax.all_to_all(sending, 'grid', split_axis=0, concat_axis=0, tiled=True)  14.9 us
    all_to_all x1, waiting for transfers between devices, sent_to_all(): return lax.all_to_all(copies, axis, split_axis=0, concat_axis=0, tiled=True)  7.86 us
    dot_general x1, matrix products, local(): lax.dot_general(onehot, arrived, (((0,), (0,)), ((), ())), precision=lax....  6.95 us
  transfers between devices with their start and end apart: 3, of which 2 were waited for; matrix products, arithmetic and copies ran while one was open for 22% of the time, Pallas kernels for 0%

commit v1 on v0

v1 whole, which is shorter than its diff:
```python
import jax
import jax.numpy as jnp
from jax import lax
from jax.experimental import pallas as pl
from jax.experimental.pallas import tpu as pltpu
from jax.sharding import PartitionSpec as P
import math

BLK = 128
NB = 4
LANES = 128
HALVES = 2

kappa_pbe = 0.804
mu_coef = 0.2195
slater = -0.7385587663820224
grad_scale = 4.0 * (3.0 * math.pi**2) ** (2.0 / 3.0)
soft_square = 0.25

SMEM = pl.BlockSpec(memory_space=pltpu.SMEM)
VMEM = pl.BlockSpec(memory_space=pltpu.VMEM)


def owner_of(table, column, batch):
    return lax.shift_right_logical(table[column, batch], 1)


def pack_kernel(place, table, counts, coords, out, tiles):
    first = place[0] * NB
    columns = table.shape[0]
    out[...] = jnp.zeros_like(out)
    for batch in range(NB):
        count = jnp.full((1, LANES), counts[batch].astype(jnp.float32), jnp.float32)
        for half in range(HALVES):
            for comp in range(3):
                tiles[batch, pl.ds(half * 4 + comp, 1), :] = coords[
                    comp, pl.ds(batch, 1), pl.ds(half * LANES, LANES)
                ]
            tiles[batch, pl.ds(half * 4 + 3, 1), :] = count
    for batch in range(NB):
        tile = tiles[batch]
        for column in range(columns):
            out[owner_of(table, column, first + batch)] = tile


def params_kernel(place, centres, exponents, rows_out, cols_out, tile):
    tile[...] = jnp.zeros_like(tile)

    def fill(block, out, slot):
        start = pl.multiple_of(block * BLK, BLK)
        tile[pl.ds(0, 3), :] = centres[:, pl.ds(start, BLK)]
        tile[pl.ds(3, 1), :] = exponents[pl.ds(block, 1), :]
        out[pl.ds(pl.multiple_of(slot * BLK, BLK), BLK), :] = tile[...].T

    row_blocks = rows_out.shape[0] // BLK
    col_blocks = cols_out.shape[0] // BLK
    for slot in range(row_blocks):
        fill(place[0] * row_blocks + slot, rows_out, slot)
    for slot in range(col_blocks):
        fill(place[1] * col_blocks + slot, cols_out, slot)


def offsets_of(params, point):
    return [point[comp] - params[:, comp : comp + 1] for comp in range(3)]


def values_of(params, offset):
    distance = offset[0] * offset[0] + offset[1] * offset[1] + offset[2] * offset[2]
    return jnp.exp(distance * (-params[:, 3:4]))


def total_rows(array):
    return jnp.sum(array, axis=0, keepdims=True)


def decode(entry):
    half = entry & 1
    block = lax.shift_right_logical(entry, 1) & 15
    row = lax.shift_right_logical(entry, 5) & 1
    source = lax.shift_right_logical(entry, 6)
    return source, row, block, half


def density_kernel(
    place, table, arrived, row_params, col_params, density, out, work, *, group
):
    rank = place[0]
    column = place[1]
    own = rank // group
    sources = arrived.shape[0]
    col_blocks = col_params.shape[0] // BLK
    out[...] = jnp.zeros_like(out)

    def list_source(source, filled):
        choice = jnp.int32(0)
        chosen = jnp.int32(0)
        found = jnp.int32(0)
        for batch in range(NB):
            block = table[own, source * NB + batch]
            match = lax.shift_right_logical(block, 1) == rank
            choice = jnp.where(match, source * NB + batch, choice)
            chosen = jnp.where(match, block, chosen)
            found = jnp.where(match, 1, found)
        target = table[column, choice] - column * col_blocks
        entry = source * 64 + (chosen & 1) * 32 + target * 2
        count = arrived[source, 3:4, :][0, 0]
        work[filled + 1] = entry
        filled = filled + found
        work[filled + 1] = entry + 1
        return filled + jnp.where(count > LANES, found, 0)

    filled = lax.fori_loop(0, sources, list_source, jnp.int32(0))
    work[0] = filled

    @pl.when((filled & 1) == 1)
    def _():
        work[filled + 1] = work[filled]

    def partial_sums(entry):
        source, row, block, half = decode(entry)
        point = [arrived[source, pl.ds(half * 4 + comp, 1), :] for comp in range(3)]
        row_start = pl.multiple_of(row * BLK, BLK)
        col_start = pl.multiple_of(block * BLK, BLK)
        rows = row_params[pl.ds(row_start, BLK), :]
        cols = col_params[pl.ds(col_start, BLK), :]
        tile = density[pl.ds(row_start, BLK), pl.ds(col_start, BLK)]
        row_offset = offsets_of(rows, point)
        row_values = values_of(rows, row_offset)
        col_offset = offsets_of(cols, point)
        col_values = values_of(cols, col_offset)
        right = lax.dot_general(
            tile,
            row_values.astype(jnp.bfloat16),
            (((0,), (0,)), ((), ())),
            preferred_element_type=jnp.float32,
        )
        left = lax.dot_general(
            tile,
            col_values.astype(jnp.bfloat16),
            (((1,), (0,)), ((), ())),
            preferred_element_type=jnp.float32,
        )
        col_product = col_values * right
        row_slope = (row_values * left) * (-2.0 * rows[:, 3:4])
        col_slope = col_product * (-2.0 * cols[:, 3:4])
        sums = [total_rows(col_product)]
        for comp in range(3):
            sums.append(total_rows(row_offset[comp] * row_slope + col_offset[comp] * col_slope))
        return source, half, sums

    def pair(step, carry):
        results = [partial_sums(work[2 * step + unit + 1]) for unit in range(2)]
        for source, half, sums in results:
            for comp in range(4):
                out[source, pl.ds(half * 4 + comp, 1), :] = sums[comp]
        return carry

    lax.fori_loop(0, (filled + 1) // 2, pair, 0)


def collect_kernel(place, table, arrived, out):
    first = place[0] * NB
    columns = table.shape[0]
    for batch in range(NB):
        total = arrived[owner_of(table, 0, first + batch)]
        for column in range(1, columns):
            total = total + arrived[owner_of(table, column, first + batch)]
        for copy in range(out.shape[0]):
            out[copy, batch] = total


def point_kernel(
    place, table, counts, partial, weights, core, out, charge_out, energy_out, summed, tiles, scale
):
    first = place[0] * NB
    columns = table.shape[0]
    for batch in range(NB):
        total = partial[0, batch]
        for column in range(1, partial.shape[0]):
            total = total + partial[column, batch]
        summed[pl.ds(batch * 8, 8), :] = total
    lane = lax.broadcasted_iota(jnp.int32, (1, LANES), 1)
    for batch in range(NB):
        for half in range(HALVES):
            place_row = pl.ds(batch * HALVES + half, 1)
            live = jnp.where(lane + half * LANES < counts[batch], 1.0, 0.0).astype(jnp.float32)
            scale[0, place_row, :] = live
            scale[1, place_row, :] = weights[pl.ds(batch, 1), pl.ds(half * LANES, LANES)]
            scale[2, place_row, :] = core[pl.ds(batch, 1), pl.ds(half * LANES, LANES)]
    live = scale[0]
    point_scale = scale[1] * live
    count_rows = NB * HALVES
    valence = live * summed[pl.ds(0, count_rows, stride=4), :]
    gradient = [live * summed[pl.ds(comp + 1, count_rows, stride=4), :] for comp in range(3)]
    grad_square = (
        gradient[0] * gradient[0] + gradient[1] * gradient[1] + gradient[2] * gradient[2]
    )
    total = valence + scale[2]
    root = jnp.sqrt(total * total + soft_square)
    regular = 0.5 * (total + root)
    third = jnp.exp(jnp.log(regular) * (1.0 / 3.0))
    four_thirds = regular * third
    scaled = grad_scale * four_thirds * four_thirds
    weighted = mu_coef * grad_square
    inverse = 1.0 / (kappa_pbe * scaled + weighted)
    fraction = scaled * inverse
    enhance = 1.0 + kappa_pbe - kappa_pbe * kappa_pbe * fraction
    energy = slater * four_thirds * enhance
    square = kappa_pbe * kappa_pbe * mu_coef
    deriv_sigma = slater * four_thirds * (square * fraction * inverse)
    enhance_slope = (
        -(kappa_pbe * kappa_pbe)
        * (weighted * inverse)
        * inverse
        * (grad_scale * (8.0 / 3.0) * four_thirds * third)
    )
    deriv_regular = slater * ((4.0 / 3.0) * third * enhance + four_thirds * enhance_slope)
    deriv_density = deriv_regular * (0.5 * (1.0 + total / root))
    fweight = point_scale * deriv_density
    factor = 2.0 * point_scale * deriv_sigma
    results = [fweight] + [factor * gradient[comp] for comp in range(3)]
    tiles[pl.ds(0, count_rows, stride=4), :] = results[0]
    for comp in range(3):
        tiles[pl.ds(comp + 1, count_rows, stride=4), :] = results[comp + 1]
    out[...] = jnp.zeros_like(out)
    for batch in range(NB):
        tile = tiles[pl.ds(batch * 8, 8), :]
        for column in range(columns):
            out[owner_of(table, column, first + batch)] = tile
    scale[0] = valence
    scale[1] = point_scale * energy
    for batch in range(NB):
        for half in range(HALVES):
            charge_out[pl.ds(batch, 1), pl.ds(half * LANES, LANES)] = scale[
                0, pl.ds(batch * HALVES + half, 1), :
            ]
        energy_out[batch] = jnp.sum(scale[1, pl.ds(batch * HALVES, HALVES), :])


def potential_kernel(work, arrived, factors, row_params, col_params, out):
    out[...] = jnp.zeros_like(out)
    filled = work[0]

    def tile_of(entry, keep):
        source, row, block, half = decode(entry)
        point = [arrived[source, pl.ds(half * 4 + comp, 1), :] for comp in range(3)]
        factor = [factors[source, pl.ds(half * 4 + comp, 1), :] * keep for comp in range(4)]
        row_start = pl.multiple_of(row * BLK, BLK)
        col_start = pl.multiple_of(block * BLK, BLK)

        def sides(params):
            offset = offsets_of(params, point)
            values = values_of(params, offset)
            along = (
                factor[1] * offset[0] + factor[2] * offset[1] + factor[3] * offset[2]
            ) * (-2.0 * params[:, 3:4])
            return values, along * values

        row_values, row_across = sides(row_params[pl.ds(row_start, BLK), :])
        col_values, col_across = sides(col_params[pl.ds(col_start, BLK), :])
        along = factor[0] * col_values + col_across
        left_side = jnp.concatenate(
            [row_values.astype(jnp.bfloat16), row_across.astype(jnp.bfloat16)], axis=1
        )
        right_side = jnp.concatenate(
            [along.astype(jnp.bfloat16), col_values.astype(jnp.bfloat16)], axis=1
        )
        product = lax.dot_general(
            left_side,
            right_side,
            (((1,), (1,)), ((), ())),
            preferred_element_type=jnp.float32,
        )
        return row_start, col_start, product

    def pair(step, carry):
        results = []
        for unit in range(2):
            index = 2 * step + unit
            keep = jnp.where(index < filled, 1.0, 0.0).astype(jnp.float32)
            results.append(tile_of(work[index + 1], keep))
        for row_start, col_start, product in results:
            place = (pl.ds(row_start, BLK), pl.ds(col_start, BLK))
            out[place] = out[place] + product
        return carry

    lax.fori_loop(0, (filled + 1) // 2, pair, 0)


def local(density, centres, exponents, coords, weights, core_density, counts, blocks):
    sources = lax.axis_size("grid")
    columns = lax.axis_size("col")
    rows, cols = density.shape
    points = coords.shape[2]
    f32 = jnp.float32
    params = pltpu.CompilerParams(vmem_limit_bytes=48 * 1024 * 1024)
    place = jnp.stack([lax.axis_index("grid"), lax.axis_index("col")]).astype(jnp.int32)
    table = blocks.T
    slots = jax.ShapeDtypeStruct((sources, 8, LANES), f32)

    outgoing = pl.pallas_call(
        pack_kernel,
        out_shape=slots,
        in_specs=[SMEM, SMEM, SMEM, VMEM],
        out_specs=VMEM,
        scratch_shapes=[pltpu.VMEM((NB, 8, LANES), f32)],
        compiler_params=params,
        name="pack",
    )(place, table, counts, coords.transpose(1, 0, 2))
    arrived = lax.all_to_all(outgoing, "grid", split_axis=0, concat_axis=0, tiled=True)
    row_params, col_params = pl.pallas_call(
        params_kernel,
        out_shape=(jax.ShapeDtypeStruct((rows, 8), f32), jax.ShapeDtypeStruct((cols, 8), f32)),
        in_specs=[SMEM, VMEM, VMEM],
        out_specs=(VMEM, VMEM),
        scratch_shapes=[pltpu.VMEM((8, LANES), f32)],
        compiler_params=params,
        name="params",
    )(place, centres, exponents.reshape(-1, LANES))
    partial, work = pl.pallas_call(
        lambda *refs: density_kernel(*refs, group=sources // columns),
        out_shape=(slots, jax.ShapeDtypeStruct((2 * sources + 8,), jnp.int32)),
        in_specs=[SMEM, SMEM, VMEM, VMEM, VMEM, VMEM],
        out_specs=(VMEM, SMEM),
        compiler_params=params,
        name="density",
    )(place, table, arrived, row_params, col_params, density)
    returned = lax.all_to_all(partial, "grid", split_axis=0, concat_axis=0, tiled=True)
    copies = pl.pallas_call(
        collect_kernel,
        out_shape=jax.ShapeDtypeStruct((columns, NB, 8, LANES), f32),
        in_specs=[SMEM, SMEM, VMEM],
        out_specs=VMEM,
        compiler_params=params,
        name="collect",
    )(place, table, returned)
    everything = lax.all_to_all(copies, "col", split_axis=0, concat_axis=0, tiled=True)
    sending, orbital_charge_samples, xc_batch_amounts = pl.pallas_call(
        point_kernel,
        out_shape=(
            slots,
            jax.ShapeDtypeStruct((NB, points), f32),
            jax.ShapeDtypeStruct((NB,), f32),
        ),
        in_specs=[SMEM, SMEM, SMEM, VMEM, VMEM, VMEM],
        out_specs=(VMEM, VMEM, SMEM),
        scratch_shapes=[
            pltpu.VMEM((NB * 8, LANES), f32),
            pltpu.VMEM((NB * 8, LANES), f32),
            pltpu.VMEM((3, 8, LANES), f32),
        ],
        compiler_params=params,
        name="points",
    )(place, table, counts, everything, weights, core_density)
    factors = lax.all_to_all(sending, "grid", split_axis=0, concat_axis=0, tiled=True)
    potential_matrix_xc = pl.pallas_call(
        potential_kernel,
        out_shape=jax.ShapeDtypeStruct((rows, cols), f32),
        in_specs=[SMEM, VMEM, VMEM, VMEM, VMEM],
        out_specs=VMEM,
        compiler_params=params,
        name="potential",
    )(work, arrived, factors, row_params, col_params)
    return (potential_matrix_xc, orbital_charge_samples, xc_batch_amounts)


def solution(mesh):
    return jax.shard_map(
        local,
        mesh=mesh,
        in_specs=(
            P("grid", "col"),
            P(),
            P(),
            P("grid", None, None),
            P("grid", None),
            P("grid", None),
            P("grid"),
            P(),
        ),
        out_specs=(P("grid", "col"), P("grid", None), P("grid")),
        check_vma=False,
    )
```

time: 293 us -> 121 us (0.41); the launches traced: 288 us -> 119 us
  local copies, waits for them, and re-layouts: 107 us -> 5.78 us
  waiting for transfers between devices: 103 us -> 10.3 us
  blocking collectives: 0 us -> 54.4 us
  Pallas kernels: 0 us -> 32.9 us
  other arithmetic: 25.2 us -> 0.08 us
  starting transfers between devices: 36.7 us -> 14.8 us
  matrix products: 11.5 us -> 0 us
  between operations: 3.81 us -> 0.7 us
    all_to_all x2 -> x0, waiting for transfers between devices: 103 us -> none  [the longest x1 94.7 us: local(): lax.all_to_all(sending, 'grid', split_axis=0, concat_axis=0, tiled=True)]
    gather x10 -> x0, local copies, waits for them, and re-layouts: 57.3 us -> none  [the longest x4 28.3 us: local(): centre_rows = jnp.take(centres, func_index, axis=1)]
    all_to_all x0 -> x3, blocking collectives: none -> 54.4 us  [the longest x1 20.7 us: local(): lax.all_to_all(partial, 'grid', split_axis=0, concat_axis=0, tiled=True)]
    pallas_call x0 -> x6, Pallas kernels: none -> 32.9 us  [the longest x1 15.5 us: local(): pl.pallas_call(lambda *refs: density_kernel(*refs, group=sources // colum...]
    all_to_all x2 -> x0, starting transfers between devices: 21.7 us -> none  [the longest x1 14.9 us: local(): lax.all_to_all(sending, 'grid', split_axis=0, concat_axis=0, tiled=True)]
    unnamed x34 -> x20, local copies, waits for them, and re-layouts: 27 us -> 5.78 us
    dot_general x16 -> x0, matrix products: 11.5 us -> none  [the longest x1 6.95 us: local(): lax.dot_general(onehot, arrived, (((0,), (0,)), ((), ())), precision=lax....]
    all_to_all x1, waiting for transfers between devices: 0.01 us -> 10.3 us  [local(): lax.all_to_all(outgoing, 'grid', split_axis=0, concat_axis=0, tiled=True)]
  transfers between devices with their start and end apart: 3 -> 1, of which waited for: 2 -> 1; matrix products, arithmetic and copies ran while one was open for 22% -> 0% of each run, Pallas kernels for 0% -> 1%
where the time goes in v1:
time: 121 us; the launch traced here: 119 us
  blocking collectives  54.4 us (45%)
  Pallas kernels  32.9 us (27%)
  starting transfers between devices  14.8 us (12%)
  waiting for transfers between devices  10.3 us (9%)
  local copies, waits for them, and re-layouts  5.78 us (5%)
    all_to_all x1, blocking collectives, local(): lax.all_to_all(partial, 'grid', split_axis=0, concat_axis=0, tiled=True)  20.7 us
    all_to_all x1, blocking collectives, local(): lax.all_to_all(sending, 'grid', split_axis=0, concat_axis=0, tiled=True)  19 us
    pallas_call x1, Pallas kernels, local(): pl.pallas_call(lambda *refs: density_kernel(*refs, group=sources // colum...  15.5 us
    all_to_all x1, starting transfers between devices, local(): lax.all_to_all(outgoing, 'grid', split_axis=0, concat_axis=0, tiled=True)  14.8 us
    all_to_all x1, blocking collectives, local(): lax.all_to_all(copies, 'col', split_axis=0, concat_axis=0, tiled=True)  14.7 us
    pallas_call x1, Pallas kernels, local(): pl.pallas_call(potential_kernel, out_shape=jax.ShapeDtypeStruct((rows, co...  12.9 us
    all_to_all x1, waiting for transfers between devices, local(): lax.all_to_all(outgoing, 'grid', split_axis=0, concat_axis=0, tiled=True)  10.3 us
    unnamed x20, local copies, waits for them, and re-layouts  5.78 us
  transfers between devices with their start and end apart: 1, of which 1 were waited for; matrix products, arithmetic and copies ran while one was open for 0% of the time, Pallas kernels for 1%

profile of v1, /device:TPU:1, one launch (start us, length us, event | category | flops | bytes accessed | tf_op | source)
XLA Modules:
  0.0 119.1 jit_solution(10074188201963279294)
XLA Ops:
  0.6 0.1 pad_add_fusion.place.refs_0_
  0.7 0.0 copy-start.2
  0.7 0.7 copy-done.2
  1.4 0.0 copy-start.5
  1.4 0.7 copy-done.5
  2.1 0.0 copy-start.8
  2.1 0.7 copy-done.8
  2.8 1.4 %pack.1 = f32[64,8,128]{2,1,0:T(8,128)} custom-call(s32[2]{0:T(128)S(1)} %pad_add_fusion.place.refs_0_, s32[8,256]{1,0:T(8,128)S(1)} %bitcast.5, s32[4]{0:T(128)S(1)} %copy-done.8, f32[3,4,256]{2,1,0:T(4,128)S(1)} %bitcast.10), custom_call_target="tpu_custom_call" | custom-call | tf_op jit(solution)/shard_map/pack/pallas_call | solution.py:301
  4.2 14.8 %all-to-all-start = ((f32[64,8,128]{2,1,0:T(8,128)}), f32[64,8,128]{2,1,0:T(8,128)S(1)}, u32[]{:S(2)}, u32[]{:S(2)}) async-start(f32[64,8,128]{2,1,0:T(8,128)} %pack.1), calls=%async_computation | async-start | bytes 524288 | tf_op jit(solution)/shard_map/all_to_all | solution.py:310
  19.0 0.0 copy-start.9
  19.1 0.0 copy-start.1
  19.1 0.9 copy-done.1
  20.0 0.0 copy-start.4
  20.0 0.8 copy-done.4
  20.9 0.0 copy-start.6
  20.9 0.0 copy-start.7
  20.9 0.9 params.1
  21.8 10.3 %all-to-all-done.refs_2_.arrived = f32[64,8,128]{2,1,0:T(8,128)S(1)} async-done(((f32[64,8,128]{2,1,0:T(8,128)}), f32[64,8,128]{2,1,0:T(8,128)S(1)}, u32[]{:S(2)}, u32[]{:S(2)}) %all-to-all-start) | async-done | bytes 262176 | tf_op jit(solution)/shard_map/all_to_all | solution.py:310
  32.1 0.0 copy-start
  32.1 1.2 %copy-done = bf16[256,2048]{1,0:T(8,128)(2,1)S(1)} copy-done((bf16[256,2048]{1,0:T(8,128)(2,1)S(1)}, bf16[256,2048]{1,0:T(8,128)(2,1)}, u32[]{:S(2)}) %copy-start) | copy-done | bytes 1048600
  33.3 0.0 copy-start.3
  33.4 0.7 copy-done.3
  34.0 15.5 %density.1 = (f32[64,8,128]{2,1,0:T(8,128)S(1)}, s32[136]{0:T(256)S(1)}) custom-call(s32[2]{0:T(128)S(1)} %pad_add_fusion.place.refs_0_, s32[8,256]{1,0:T(8,128)S(1)} %bitcast.6, f32[64,8,128]{2,1,0:T(8,128)S(1)} %all-to-all-done.refs_2_.arrived, f32[256,8]{1,0:T(8,128)S(1)} %get-tuple-element.10.refs_3_.row_params, ...), custom_call_target="tpu_custom_call" | custom-call | tf_op jit(solution)/shard_map/density/pallas_call | solution.py:320
  49.6 20.7 %all_to_all.20.arrived = f32[64,8,128]{2,1,0:T(8,128)S(1)} all-to-all(f32[64,8,128]{2,1,0:T(8,128)S(1)} %get-tuple-element.13), channel_id=1, replica_groups=mesh['grid'=64,'col'=8] {'grid'}, dimensions={0} | all-to-all | bytes 524288 | tf_op jit(solution)/shard_map/all_to_all | solution.py:328
  70.3 0.7 collect.1
  71.0 14.7 %all_to_all.21.partial = f32[8,4,8,128]{3,2,1,0:T(8,128)S(1)} all-to-all(f32[8,4,8,128]{3,2,1,0:T(8,128)S(1)} %collect.1), channel_id=1, replica_groups=mesh['grid'=64,'col'=8] {'col'}, dimensions={0} | all-to-all | bytes 262144 | tf_op jit(solution)/shard_map/all_to_all | solution.py:337
  85.7 0.0 copy-done.9
  85.7 0.0 copy-done.6
  85.7 0.0 copy-done.7
  85.7 1.4 %points.1 = (f32[64,8,128]{2,1,0:T(8,128)S(1)}, f32[4,256]{1,0:T(4,128)}, f32[4]{0:T(128)}) custom-call(s32[2]{0:T(128)S(1)} %pad_add_fusion.place.refs_0_, s32[8,256]{1,0:T(8,128)S(1)} %bitcast.8, s32[4]{0:T(128)S(1)} %copy-done.9, f32[8,4,8,128]{3,2,1,0:T(8,128)S(1)} %all_to_all.21.partial, f32[4,256]{1,0:T(4,128)S(1)} %copy-done.6, f32[4,256]{1,0:T(4,128)S(1)} %copy-done.7), custom_call_target="tpu_custom_call" | custom-call | tf_op jit(solution)/shard_map/points/pallas_call | solution.py:338
  87.1 19.0 %all_to_all.22.factors = f32[64,8,128]{2,1,0:T(8,128)S(1)} all-to-all(f32[64,8,128]{2,1,0:T(8,128)S(1)} %get-tuple-element.14), channel_id=1, replica_groups=mesh['grid'=64,'col'=8] {'grid'}, dimensions={0} | all-to-all | bytes 524288 | tf_op jit(solution)/shard_map/all_to_all | solution.py:355
  106.2 12.9 %potential.1 = f32[256,2048]{1,0:T(8,128)} custom-call(s32[136]{0:T(256)S(1)} %get-tuple-element.12.work, f32[64,8,128]{2,1,0:T(8,128)S(1)} %all-to-all-done.refs_2_.arrived, f32[64,8,128]{2,1,0:T(8,128)S(1)} %all_to_all.22.factors, f32[256,8]{1,0:T(8,128)S(1)} %get-tuple-element.10.refs_3_.row_params, f32[2048,8]{1,0:T(8,128)S(1)} %get-tuple-element.11.refs_4_.col_params), custom_call_target="tpu_custom_call" | custom-call | tf_op jit(solution)/shard_map/potential/pallas_call | solution.py:356
Async XLA Ops:
  0.7 0.7 copy-start.2
  1.4 0.7 copy-start.5
  2.1 0.7 copy-start.8
  4.2 27.9 %all-to-all-start = ((f32[64,8,128]{2,1,0:T(8,128)}), f32[64,8,128]{2,1,0:T(8,128)S(1)}, u32[]{:S(2)}, u32[]{:S(2)}) async-start(f32[64,8,128]{2,1,0:T(8,128)} %pack.1), calls=%async_computation | async-start | bytes 524288 | tf_op jit(solution)/shard_map/all_to_all | solution.py:310
  19.0 66.7 %copy-start.9 = (s32[4]{0:T(128)S(1)}, s32[4]{0:T(128)}, u32[]{:S(2)}) copy-start(s32[4]{0:T(128)} %counts.3) | copy-start | bytes 52
  19.1 1.0 copy-start.1
  20.0 0.8 copy-start.4
  20.9 64.9 %copy-start.6 = (f32[4,256]{1,0:T(4,128)S(1)}, f32[4,256]{1,0:T(4,128)}, u32[]{:S(2)}) copy-start(f32[4,256]{1,0:T(4,128)} %weights.1) | copy-start | bytes 12292
  20.9 64.9 %copy-start.7 = (f32[4,256]{1,0:T(4,128)S(1)}, f32[4,256]{1,0:T(4,128)}, u32[]{:S(2)}) copy-start(f32[4,256]{1,0:T(4,128)} %core.1) | copy-start | bytes 12292
  32.1 1.2 %copy-start = (bf16[256,2048]{1,0:T(8,128)(2,1)S(1)}, bf16[256,2048]{1,0:T(8,128)(2,1)}, u32[]{:S(2)}) copy-start(bf16[256,2048]{1,0:T(8,128)(2,1)} %refs_5_.1) | copy-start | bytes 3145732
  33.3 0.7 copy-start.3

commit v2 on v1

v2 whole, which is shorter than its diff:
```python
from functools import partial
import math

import jax
import jax.numpy as jnp
from jax import lax
from jax.experimental import pallas as pl
from jax.experimental.pallas import tpu as pltpu
from jax.sharding import PartitionSpec as P

BLK = 128
NB = 4
LANES = 128
HALVES = 2

kappa_pbe = 0.804
mu_coef = 0.2195
slater = -0.7385587663820224
grad_scale = 4.0 * (3.0 * math.pi**2) ** (2.0 / 3.0)
soft_square = 0.25

SMEM = pl.BlockSpec(memory_space=pltpu.SMEM)
VMEM = pl.BlockSpec(memory_space=pltpu.VMEM)


LOG2E = math.log2(math.e)
SLOPE = 2.0 * math.log(2.0)
HBM = pl.BlockSpec(memory_space=pltpu.HBM)


def pack_kernel(table_hbm, counts_hbm, coords_hbm, out, slots, table, counts, coords, tiles, sems):
    copies = [
        pltpu.make_async_copy(source, target, sems.at[index])
        for index, (source, target) in enumerate(
            [(table_hbm, table), (counts_hbm, counts), (coords_hbm, coords)]
        )
    ]
    for copy in copies:
        copy.start()
    first = lax.axis_index("grid") * NB
    columns = table.shape[0]
    out[...] = jnp.zeros_like(out)
    for copy in copies:
        copy.wait()
    for batch in range(NB):
        count = jnp.full((1, LANES), counts[batch].astype(jnp.float32), jnp.float32)
        for half in range(HALVES):
            for comp in range(3):
                tiles[batch, pl.ds(half * 4 + comp, 1), :] = coords[
                    comp, pl.ds(batch, 1), pl.ds(half * LANES, LANES)
                ]
            tiles[batch, pl.ds(half * 4 + 3, 1), :] = count
    for batch in range(NB):
        tile = tiles[batch]
        for column in range(columns):
            slot = lax.shift_right_logical(table[column, first + batch], 1)
            slots[column * NB + batch] = slot
            out[slot] = tile


def prepare_kernel(table, centres, exponents, density, at_x, at_y, at_z, rate, forward, backward, work, tile, *, group):
    rank = lax.axis_index("grid")
    column = lax.axis_index("col")
    own = rank // group
    row_blocks = density.shape[0] // BLK
    col_blocks = density.shape[1] // BLK
    sources = table.shape[1] // NB
    basis = (at_x, at_y, at_z, rate)
    tile[...] = jnp.zeros_like(tile)

    def fill(block, slot):
        start = pl.multiple_of(block * BLK, BLK)
        tile[pl.ds(0, 3), :] = centres[:, pl.ds(start, BLK)]
        tile[pl.ds(3, 1), :] = exponents[pl.ds(block, 1), :] * (-LOG2E)
        upright = tile[...].T
        for comp in range(4):
            basis[comp][slot] = jnp.broadcast_to(upright[:, comp : comp + 1], (BLK, LANES))

    for slot in range(row_blocks):
        fill(rank * row_blocks + slot, slot)

    def fill_column(slot, carry):
        fill(column * col_blocks + slot, row_blocks + slot)
        start = pl.multiple_of(slot * BLK, BLK)
        for row in range(row_blocks):
            piece = density[pl.ds(row * BLK, BLK), pl.ds(start, BLK)]
            forward[slot, row] = piece
            backward[slot, row] = piece.T
        return carry

    lax.fori_loop(0, col_blocks, fill_column, 0)

    def list_sources(step, filled):
        for unit in range(4):
            source = step * 4 + unit
            code = jnp.int32(0)
            for batch in range(NB):
                part = table[own, source * NB + batch] ^ (2 * rank)
                code = jnp.where(part < 2, 8 + 2 * batch + part, code)
            choice = lax.shift_right_logical(code, 1) & 3
            target = table[column, source * NB + choice] - column * col_blocks
            work[filled + 1] = source * 64 + (code & 1) * 32 + target * 2
            filled = filled + lax.shift_right_logical(code, 3)
        return filled

    filled = lax.fori_loop(0, sources // 4, list_sources, jnp.int32(0))
    work[0] = filled
    work[filled + 1] = work[jnp.maximum(filled, 1)]


def total_rows(array):
    return jnp.sum(array, axis=0, keepdims=True)


def decode(entry):
    half = entry & 1
    block = lax.shift_right_logical(entry, 1) & 15
    row = lax.shift_right_logical(entry, 5) & 1
    source = lax.shift_right_logical(entry, 6)
    return source, row, block, half


def values_of(side, point):
    offset = [point[comp] - side(comp) for comp in range(3)]
    distance = offset[0] * offset[0] + offset[1] * offset[1] + offset[2] * offset[2]
    return jnp.exp2(distance * side(3))


def over_pairs(work, handle, carry):
    filled = work[0]

    def pair(step, carry):
        entries = [(work[2 * step + unit + 1], 2 * step + unit < filled) for unit in range(2)]
        return handle(entries, carry)

    return lax.fori_loop(0, lax.shift_right_logical(filled + 1, 1), pair, carry)


def density_kernel(work, arrived, at_x, at_y, at_z, rate, forward, backward, out, later):
    basis = (at_x, at_y, at_z, rate)
    row_blocks = forward.shape[1]
    out[...] = jnp.zeros_like(out)

    def partial_sums(entry):
        source, row, block, half = decode(entry)
        point = [arrived[source, pl.ds(half * 4 + comp, 1), :] for comp in range(3)]

        def row_side(comp):
            return basis[comp][row]

        def col_side(comp):
            return basis[comp][row_blocks + block]

        row_values = values_of(row_side, point)
        col_values = values_of(col_side, point)
        right = jnp.dot(
            backward[block, row], row_values.astype(jnp.bfloat16), preferred_element_type=jnp.float32
        )
        left = jnp.dot(
            forward[block, row], col_values.astype(jnp.bfloat16), preferred_element_type=jnp.float32
        )
        col_product = col_values * right
        col_slope = col_product * col_side(3)
        row_slope = row_values * left * row_side(3)
        slope = total_rows(row_slope + col_slope)
        sums = [total_rows(col_product)]
        for comp in range(3):
            moment = total_rows(row_slope * row_side(comp) + col_slope * col_side(comp))
            sums.append(SLOPE * (point[comp] * slope - moment))
        return source, half, sums

    def first_halves(entries, filled):
        for entry, real in entries:
            count = arrived[lax.shift_right_logical(entry, 6), 3:4, :][0, 0]
            later[filled + 1] = entry + 1
            filled = filled + jnp.where(jnp.logical_and(count > LANES, real), 1, 0)
        return halves(entries, filled)

    def halves(entries, carry):
        results = [partial_sums(entry) for entry, _ in entries]
        for source, half, sums in results:
            for comp in range(4):
                out[source, pl.ds(half * 4 + comp, 1), :] = sums[comp]
        return carry

    filled = over_pairs(work, first_halves, jnp.int32(0))
    later[0] = filled
    later[filled + 1] = later[jnp.maximum(filled, 1)]
    over_pairs(later, halves, 0)


def collect_kernel(slots, arrived, out):
    columns = slots.shape[0] // NB
    for batch in range(NB):
        total = arrived[slots[batch]]
        for column in range(1, columns):
            total = total + arrived[slots[column * NB + batch]]
        for copy in range(out.shape[0]):
            out[copy, batch] = total


def point_kernel(
    slots, counts, sums, weights, core, out, charge_out, energy_out, summed, tiles, scale
):
    columns = slots.shape[0] // NB
    for batch in range(NB):
        total = sums[0, batch]
        for column in range(1, sums.shape[0]):
            total = total + sums[column, batch]
        summed[pl.ds(batch * 8, 8), :] = total
    lane = lax.broadcasted_iota(jnp.int32, (1, LANES), 1)
    for batch in range(NB):
        for half in range(HALVES):
            place_row = pl.ds(batch * HALVES + half, 1)
            live = jnp.where(lane + half * LANES < counts[batch], 1.0, 0.0).astype(jnp.float32)
            scale[0, place_row, :] = live
            scale[1, place_row, :] = weights[pl.ds(batch, 1), pl.ds(half * LANES, LANES)]
            scale[2, place_row, :] = core[pl.ds(batch, 1), pl.ds(half * LANES, LANES)]
    live = scale[0]
    point_scale = scale[1] * live
    count_rows = NB * HALVES
    valence = live * summed[pl.ds(0, count_rows, stride=4), :]
    gradient = [live * summed[pl.ds(comp + 1, count_rows, stride=4), :] for comp in range(3)]
    grad_square = (
        gradient[0] * gradient[0] + gradient[1] * gradient[1] + gradient[2] * gradient[2]
    )
    total = valence + scale[2]
    root = jnp.sqrt(total * total + soft_square)
    regular = 0.5 * (total + root)
    third = jnp.exp(jnp.log(regular) * (1.0 / 3.0))
    four_thirds = regular * third
    scaled = grad_scale * four_thirds * four_thirds
    weighted = mu_coef * grad_square
    inverse = 1.0 / (kappa_pbe * scaled + weighted)
    fraction = scaled * inverse
    enhance = 1.0 + kappa_pbe - kappa_pbe * kappa_pbe * fraction
    energy = slater * four_thirds * enhance
    square = kappa_pbe * kappa_pbe * mu_coef
    deriv_sigma = slater * four_thirds * (square * fraction * inverse)
    enhance_slope = (
        -(kappa_pbe * kappa_pbe)
        * (weighted * inverse)
        * inverse
        * (grad_scale * (8.0 / 3.0) * four_thirds * third)
    )
    deriv_regular = slater * ((4.0 / 3.0) * third * enhance + four_thirds * enhance_slope)
    deriv_density = deriv_regular * (0.5 * (1.0 + total / root))
    fweight = point_scale * deriv_density
    factor = 2.0 * point_scale * deriv_sigma
    results = [fweight] + [factor * gradient[comp] for comp in range(3)]
    tiles[pl.ds(0, count_rows, stride=4), :] = results[0]
    for comp in range(3):
        tiles[pl.ds(comp + 1, count_rows, stride=4), :] = results[comp + 1]
    out[...] = jnp.zeros_like(out)
    for batch in range(NB):
        tile = tiles[pl.ds(batch * 8, 8), :]
        for column in range(columns):
            out[slots[column * NB + batch]] = tile
    scale[0] = valence
    scale[1] = point_scale * energy
    for batch in range(NB):
        for half in range(HALVES):
            charge_out[pl.ds(batch, 1), pl.ds(half * LANES, LANES)] = scale[
                0, pl.ds(batch * HALVES + half, 1), :
            ]
        energy_out[batch] = jnp.sum(scale[1, pl.ds(batch * HALVES, HALVES), :])


def potential_kernel(work, later, arrived, factors, at_x, at_y, at_z, rate, out):
    basis = (at_x, at_y, at_z, rate)
    row_blocks = out.shape[0] // BLK
    out[...] = jnp.zeros_like(out)

    def tile_of(entry, real):
        source, row, block, half = decode(entry)
        keep = jnp.where(real, 1.0, 0.0).astype(jnp.float32)
        point = [arrived[source, pl.ds(half * 4 + comp, 1), :] for comp in range(3)]
        factor = [factors[source, pl.ds(half * 4 + comp, 1), :] * keep for comp in range(4)]
        push = [SLOPE * factor[comp + 1] for comp in range(3)]
        along_point = push[0] * point[0] + push[1] * point[1] + push[2] * point[2]

        def turn(side):
            along_centre = push[0] * side(0) + push[1] * side(1) + push[2] * side(2)
            return (along_point - along_centre) * side(3)

        def row_side(comp):
            return basis[comp][row]

        def col_side(comp):
            return basis[comp][row_blocks + block]

        row_values = values_of(row_side, point)
        col_values = values_of(col_side, point)
        row_across = row_values * turn(row_side)
        along = col_values * (factor[0] + turn(col_side))
        left_side = jnp.concatenate(
            [row_values.astype(jnp.bfloat16), row_across.astype(jnp.bfloat16)], axis=1
        )
        right_side = jnp.concatenate(
            [along.astype(jnp.bfloat16), col_values.astype(jnp.bfloat16)], axis=1
        )
        product = lax.dot_general(
            left_side,
            right_side,
            (((1,), (1,)), ((), ())),
            preferred_element_type=jnp.float32,
        )
        row_start = pl.multiple_of(row * BLK, BLK)
        col_start = pl.multiple_of(block * BLK, BLK)
        return row_start, col_start, product

    def handle(entries, carry):
        results = [tile_of(entry, real) for entry, real in entries]
        for row_start, col_start, product in results:
            place = (pl.ds(row_start, BLK), pl.ds(col_start, BLK))
            out[place] = out[place] + product
        return carry

    over_pairs(work, handle, 0)
    over_pairs(later, handle, 0)


def local(density, centres, exponents, coords, weights, core_density, counts, blocks):
    sources = lax.axis_size("grid")
    columns = lax.axis_size("col")
    rows, cols = density.shape
    points = coords.shape[2]
    f32 = jnp.float32
    params = pltpu.CompilerParams(vmem_limit_bytes=16 * 1024 * 1024)
    table = blocks.T
    shape = jax.ShapeDtypeStruct
    messages = shape((sources, 8, LANES), f32)
    blocks_held = rows // BLK + cols // BLK
    tile_shape = shape((cols // BLK, rows // BLK, BLK, BLK), jnp.bfloat16)
    spread = shape((blocks_held, BLK, LANES), f32)
    listed = shape((sources + 8,), jnp.int32)

    outgoing, slots = pl.pallas_call(
        pack_kernel,
        out_shape=(messages, shape((columns * NB,), jnp.int32)),
        in_specs=[HBM, HBM, HBM],
        out_specs=(VMEM, SMEM),
        scratch_shapes=[
            pltpu.SMEM(table.shape, jnp.int32),
            pltpu.SMEM(counts.shape, jnp.int32),
            pltpu.VMEM((3, NB, points), f32),
            pltpu.VMEM((NB, 8, LANES), f32),
            pltpu.SemaphoreType.DMA((3,)),
        ],
        compiler_params=params,
        name="pack",
    )(
        *[
            pltpu.with_memory_space_constraint(array, pltpu.HBM)
            for array in (table, counts, coords.transpose(1, 0, 2))
        ]
    )
    arrived = lax.all_to_all(outgoing, "grid", split_axis=0, concat_axis=0, tiled=True)
    *basis, forward, backward, work = pl.pallas_call(
        partial(prepare_kernel, group=sources // columns),
        out_shape=(spread,) * 4 + (tile_shape, tile_shape, listed),
        in_specs=[SMEM, VMEM, VMEM, VMEM],
        out_specs=(VMEM,) * 6 + (SMEM,),
        scratch_shapes=[pltpu.VMEM((8, LANES), f32)],
        compiler_params=params,
        name="prepare",
    )(table, centres, exponents.reshape(-1, LANES), density)
    partials, later = pl.pallas_call(
        density_kernel,
        out_shape=(messages, listed),
        in_specs=[SMEM] + [VMEM] * 7,
        out_specs=(VMEM, SMEM),
        compiler_params=params,
        name="density",
    )(work, arrived, *basis, forward, backward)
    returned = lax.all_to_all(partials, "grid", split_axis=0, concat_axis=0, tiled=True)
    copies = pl.pallas_call(
        collect_kernel,
        out_shape=shape((columns, NB, 8, LANES), f32),
        in_specs=[SMEM, VMEM],
        out_specs=VMEM,
        compiler_params=params,
        name="collect",
    )(slots, returned)
    everything = lax.all_to_all(copies, "col", split_axis=0, concat_axis=0, tiled=True)
    sending, orbital_charge_samples, xc_batch_amounts = pl.pallas_call(
        point_kernel,
        out_shape=(messages, shape((NB, points), f32), shape((NB,), f32)),
        in_specs=[SMEM, SMEM, VMEM, VMEM, VMEM],
        out_specs=(VMEM, VMEM, SMEM),
        scratch_shapes=[
            pltpu.VMEM((NB * 8, LANES), f32),
            pltpu.VMEM((NB * 8, LANES), f32),
            pltpu.VMEM((3, 8, LANES), f32),
        ],
        compiler_params=params,
        name="points",
    )(slots, counts, everything, weights, core_density)
    factors = lax.all_to_all(sending, "grid", split_axis=0, concat_axis=0, tiled=True)
    potential_matrix_xc = pl.pallas_call(
        potential_kernel,
        out_shape=shape((rows, cols), f32),
        in_specs=[SMEM, SMEM] + [VMEM] * 6,
        out_specs=VMEM,
        compiler_params=params,
        name="potential",
    )(work, later, arrived, factors, *basis)
    return (potential_matrix_xc, orbital_charge_samples, xc_batch_amounts)


def solution(mesh):
    return jax.shard_map(
        local,
        mesh=mesh,
        in_specs=(
            P("grid", "col"),
            P(),
            P(),
            P("grid", None, None),
            P("grid", None),
            P("grid", None),
            P("grid"),
            P(),
        ),
        out_specs=(P("grid", "col"), P("grid", None), P("grid")),
        check_vma=False,
    )
```

time: 121 us -> 112 us (0.926)
  waiting for transfers between devices: 10.3 us -> 0.01 us
  Pallas kernels: 32.9 us -> 26.8 us
  local copies, waits for them, and re-layouts: 5.78 us -> 10.4 us
  blocking collectives: 54.4 us -> 58 us
    all_to_all x1, waiting for transfers between devices: 10.3 us -> 0.01 us  [local(): lax.all_to_all(outgoing, 'grid', split_axis=0, concat_axis=0, tiled=True)]
    pallas_call x6, Pallas kernels: 32.9 us -> 26.8 us  [the longest x1 8.52 us: local(): pl.pallas_call(potential_kernel, out_shape=shape((rows, cols), f32), in_s...]
    unnamed x20 -> x28, local copies, waits for them, and re-layouts: 5.78 us -> 10.4 us
    all_to_all x1, blocking collectives: 20.7 us -> 24.2 us  [local(): lax.all_to_all(partials, 'grid', split_axis=0, concat_axis=0, tiled=True)]
  transfers between devices with their start and end apart: 1 -> 1, of which waited for: 1 -> 0; matrix products, arithmetic and copies ran while one was open for 0% -> 0% of each run, Pallas kernels for 1% -> 7%
where the time goes in v2:
time: 112 us; the launch traced here: 111 us
  blocking collectives  58 us (52%)
  Pallas kernels  26.8 us (24%)
  starting transfers between devices  15 us (13%)
  local copies, waits for them, and re-layouts  10.4 us (9%)
    all_to_all x1, blocking collectives, local(): lax.all_to_all(partials, 'grid', split_axis=0, concat_axis=0, tiled=True)  24.2 us
    all_to_all x1, blocking collectives, local(): lax.all_to_all(sending, 'grid', split_axis=0, concat_axis=0, tiled=True)  19 us
    all_to_all x1, starting transfers between devices, local(): lax.all_to_all(outgoing, 'grid', split_axis=0, concat_axis=0, tiled=True)  15 us
    all_to_all x1, blocking collectives, local(): lax.all_to_all(copies, 'col', split_axis=0, concat_axis=0, tiled=True)  14.7 us
    unnamed x28, local copies, waits for them, and re-layouts  10.4 us
    pallas_call x1, Pallas kernels, local(): pl.pallas_call(potential_kernel, out_shape=shape((rows, cols), f32), in_s...  8.52 us
    pallas_call x1, Pallas kernels, local(): pl.pallas_call(partial(prepare_kernel, group=sources // columns), out_sha...  7.44 us
    pallas_call x1, Pallas kernels, local(): pl.pallas_call(density_kernel, out_shape=(messages, listed), in_specs=[SM...  7.36 us
  transfers between devices with their start and end apart: 1, of which 0 were waited for; matrix products, arithmetic and copies ran while one was open for 0% of the time, Pallas kernels for 7%

profile of v2, /device:TPU:1, one launch (start us, length us, event | category | flops | bytes accessed | tf_op | source)
XLA Modules:
  0.0 110.9 jit_solution(14738940893588797323)
XLA Ops:
  0.6 1.6 %pack.1 = (f32[64,8,128]{2,1,0:T(8,128)}, s32[32]{0:T(128)S(1)}) custom-call(s32[8,256]{1,0:T(8,128)} %bitcast.4, s32[4]{0:T(128)} %counts.1, f32[3,4,256]{2,1,0:T(4,128)} %bitcast.6), custom_call_target="tpu_custom_call" | custom-call | tf_op jit(solution)/shard_map/pack/pallas_call | solution.py:338
  2.2 15.0 %all-to-all-start = ((f32[64,8,128]{2,1,0:T(8,128)}), f32[64,8,128]{2,1,0:T(8,128)}, u32[]{:S(2)}, u32[]{:S(2)}) async-start(f32[64,8,128]{2,1,0:T(8,128)} %get-tuple-element.18), calls=%async_computation | async-start | bytes 524288 | tf_op jit(solution)/shard_map/all_to_all | solution.py:358
  17.3 0.0 copy-start.7
  17.3 1.2 %copy-done.7 = bf16[256,2048]{1,0:T(8,128)(2,1)S(1)} copy-done((bf16[256,2048]{1,0:T(8,128)(2,1)S(1)}, bf16[256,2048]{1,0:T(8,128)(2,1)}, u32[]{:S(2)}) %copy-start.7) | copy-done | bytes 1048600
  18.5 0.0 copy-start.8
  18.5 0.9 copy-done.8
  19.5 0.0 copy-start.9
  19.5 0.8 copy-done.9
  20.3 0.0 copy-start.10
  20.3 0.7 copy-done.10
  21.0 7.4 %prepare.1 = (f32[18,128,128]{2,1,0:T(8,128)S(1)}, f32[18,128,128]{2,1,0:T(8,128)S(1)}, f32[18,128,128]{2,1,0:T(8,128)S(1)}, f32[18,128,128]{2,1,0:T(8,128)S(1)}...) custom-call(s32[8,256]{1,0:T(8,128)S(1)} %bitcast.5, ...), custom_call_target="tpu_custom_call" | custom-call | tf_op jit(solution)/shard_map/prepare/pallas_call | solution.py:359
  28.4 0.0 copy-start
  28.5 1.0 copy-done
  29.5 0.0 copy-start.3
  29.5 1.0 copy-done.3
  30.4 0.0 copy-start.5
  30.4 1.0 copy-done.5
  31.4 0.0 all-to-all-done.arrived
  31.4 0.0 copy-start.1
  31.4 1.3 %copy-done.1 = f32[18,128,128]{2,1,0:T(8,128)S(1)} copy-done((f32[18,128,128]{2,1,0:T(8,128)S(1)}, f32[18,128,128]{2,1,0:T(8,128)}, u32[]{:S(2)}) %copy-start.1) | copy-done | bytes 1179672
  32.7 0.0 copy-start.4
  32.7 1.2 %copy-done.4 = bf16[16,2,128,128]{3,2,1,0:T(8,128)(2,1)S(1)} copy-done((bf16[16,2,128,128]{3,2,1,0:T(8,128)(2,1)S(1)}, bf16[16,2,128,128]{3,2,1,0:T(8,128)(2,1)}, u32[]{:S(2)}) %copy-start.4) | copy-done | bytes 1048600
  33.9 0.0 copy-start.6
  33.9 1.2 %copy-done.6 = bf16[16,2,128,128]{3,2,1,0:T(8,128)(2,1)S(1)} copy-done((bf16[16,2,128,128]{3,2,1,0:T(8,128)(2,1)S(1)}, bf16[16,2,128,128]{3,2,1,0:T(8,128)(2,1)}, u32[]{:S(2)}) %copy-start.6) | copy-done | bytes 1048600
  35.1 0.0 copy-start.12
  35.1 0.0 copy-start.13
  35.1 7.4 %density.3 = (f32[64,8,128]{2,1,0:T(8,128)S(1)}, s32[72]{0:T(128)S(1)}) custom-call(s32[72]{0:T(128)S(1)} %get-tuple-element.17.work, f32[64,8,128]{2,1,0:T(8,128)} %all-to-all-done.arrived, f32[18,128,128]{2,1,0:T(8,128)S(1)} %get-tuple-element.19.at_x, f32[18,128,128]{2,1,0:T(8,128)S(1)} %get-tuple-element.20.at_y, ...), custom_call_target="tpu_custom_call" | custom-call | tf_op jit(solution)/shard_map/density/pallas_call | solution.py:368
  42.5 0.0 copy-start.11
  42.5 0.0 copy-start.2
  42.5 24.2 %all_to_all.20.arrived = f32[64,8,128]{2,1,0:T(8,128)S(1)} all-to-all(f32[64,8,128]{2,1,0:T(8,128)S(1)} %get-tuple-element.27), channel_id=1, replica_groups=mesh['grid'=64,'col'=8] {'grid'}, dimensions={0} | all-to-all | bytes 524288 | tf_op jit(solution)/shard_map/all_to_all | solution.py:376
  66.8 0.6 collect.1
  67.3 14.7 %all_to_all.21.sums = f32[8,4,8,128]{3,2,1,0:T(8,128)S(1)} all-to-all(f32[8,4,8,128]{3,2,1,0:T(8,128)S(1)} %collect.1), channel_id=1, replica_groups=mesh['grid'=64,'col'=8] {'col'}, dimensions={0} | all-to-all | bytes 262144 | tf_op jit(solution)/shard_map/all_to_all | solution.py:385
  82.1 0.0 copy-done.12
  82.1 0.0 copy-done.13
  82.1 0.0 copy-done.11
  82.1 1.3 %points.1 = (f32[64,8,128]{2,1,0:T(8,128)S(1)}, f32[4,256]{1,0:T(4,128)}, f32[4]{0:T(128)}) custom-call(s32[32]{0:T(128)S(1)} %get-tuple-element.26.slots, s32[4]{0:T(128)S(1)} %copy-done.13, f32[8,4,8,128]{3,2,1,0:T(8,128)S(1)} %all_to_all.21.sums, f32[4,256]{1,0:T(4,128)S(1)} %copy-done.11, f32[4,256]{1,0:T(4,128)S(1)} %copy-done.12), custom_call_target="tpu_custom_call" | custom-call | tf_op jit(solution)/shard_map/points/pallas_call | solution.py:386
  83.3 19.0 %all_to_all.22.factors = f32[64,8,128]{2,1,0:T(8,128)S(1)} all-to-all(f32[64,8,128]{2,1,0:T(8,128)S(1)} %get-tuple-element.28), channel_id=1, replica_groups=mesh['grid'=64,'col'=8] {'grid'}, dimensions={0} | all-to-all | bytes 524288 | tf_op jit(solution)/shard_map/all_to_all | solution.py:399
  102.4 0.0 copy-done.2
  102.4 8.5 %potential.1 = f32[256,2048]{1,0:T(8,128)} custom-call(s32[72]{0:T(128)S(1)} %get-tuple-element.17.work, s32[72]{0:T(128)S(1)} %get-tuple-element.25.later, f32[64,8,128]{2,1,0:T(8,128)} %all-to-all-done.arrived, f32[64,8,128]{2,1,0:T(8,128)S(1)} %all_to_all.22.factors, f32[18,128,128]{2,1,0:T(8,128)S(1)} %get-tuple-element.19.at_x, ...), custom_call_target="tpu_custom_call" | custom-call | tf_op jit(solution)/shard_map/potential/pallas_call | solution.py:400
Async XLA Ops:
  2.2 29.2 %all-to-all-start = ((f32[64,8,128]{2,1,0:T(8,128)}), f32[64,8,128]{2,1,0:T(8,128)}, u32[]{:S(2)}, u32[]{:S(2)}) async-start(f32[64,8,128]{2,1,0:T(8,128)} %get-tuple-element.18), calls=%async_computation | async-start | bytes 524288 | tf_op jit(solution)/shard_map/all_to_all | solution.py:358
  17.3 1.2 %copy-start.7 = (bf16[256,2048]{1,0:T(8,128)(2,1)S(1)}, bf16[256,2048]{1,0:T(8,128)(2,1)}, u32[]{:S(2)}) copy-start(bf16[256,2048]{1,0:T(8,128)(2,1)} %density.2) | copy-start | bytes 3145732
  18.5 0.9 copy-start.8
  19.5 0.8 copy-start.9
  20.3 0.7 copy-start.10
  28.4 1.0 copy-start
  29.5 1.0 copy-start.3
  30.4 1.0 copy-start.5
  31.4 1.3 %copy-start.1 = (f32[18,128,128]{2,1,0:T(8,128)S(1)}, f32[18,128,128]{2,1,0:T(8,128)}, u32[]{:S(2)}) copy-start(f32[18,128,128]{2,1,0:T(8,128)} %copy-done) | copy-start | bytes 3538948
  32.7 1.2 %copy-start.4 = (bf16[16,2,128,128]{3,2,1,0:T(8,128)(2,1)S(1)}, bf16[16,2,128,128]{3,2,1,0:T(8,128)(2,1)}, u32[]{:S(2)}) copy-start(bf16[16,2,128,128]{3,2,1,0:T(8,128)(2,1)} %copy-done.3) | copy-start | bytes 3145732
  33.9 1.2 %copy-start.6 = (bf16[16,2,128,128]{3,2,1,0:T(8,128)(2,1)S(1)}, bf16[16,2,128,128]{3,2,1,0:T(8,128)(2,1)}, u32[]{:S(2)}) copy-start(bf16[16,2,128,128]{3,2,1,0:T(8,128)(2,1)} %copy-done.5) | copy-start | bytes 3145732
  35.1 46.9 %copy-start.12 = (f32[4,256]{1,0:T(4,128)S(1)}, f32[4,256]{1,0:T(4,128)}, u32[]{:S(2)}) copy-start(f32[4,256]{1,0:T(4,128)} %core.1) | copy-start | bytes 12292
  35.1 46.9 %copy-start.13 = (s32[4]{0:T(128)S(1)}, s32[4]{0:T(128)}, u32[]{:S(2)}) copy-start(s32[4]{0:T(128)} %counts.1) | copy-start | bytes 52
  42.5 39.5 %copy-start.11 = (f32[4,256]{1,0:T(4,128)S(1)}, f32[4,256]{1,0:T(4,128)}, u32[]{:S(2)}) copy-start(f32[4,256]{1,0:T(4,128)} %weights.1) | copy-start | bytes 12292
  42.5 59.8 %copy-start.2 = (f32[18,128,128]{2,1,0:T(8,128)S(1)}, f32[18,128,128]{2,1,0:T(8,128)}, u32[]{:S(2)}) copy-start(f32[18,128,128]{2,1,0:T(8,128)} %copy-done) | copy-start | bytes 3538948

commit v3 on v2

--- a/solution.py
+++ b/solution.py
@@ -58,29 +58,26 @@
             out[slot] = tile
 
 
-def prepare_kernel(table, centres, exponents, density, at_x, at_y, at_z, rate, forward, backward, work, tile, *, group):
+def prepare_kernel(table, centres, exponents, density, row_params, col_params, forward, backward, work, tile, *, group):
     rank = lax.axis_index("grid")
     column = lax.axis_index("col")
     own = rank // group
     row_blocks = density.shape[0] // BLK
     col_blocks = density.shape[1] // BLK
     sources = table.shape[1] // NB
-    basis = (at_x, at_y, at_z, rate)
     tile[...] = jnp.zeros_like(tile)
 
-    def fill(block, slot):
+    def fill(block, params, slot):
         start = pl.multiple_of(block * BLK, BLK)
         tile[pl.ds(0, 3), :] = centres[:, pl.ds(start, BLK)]
         tile[pl.ds(3, 1), :] = exponents[pl.ds(block, 1), :] * (-LOG2E)
-        upright = tile[...].T
-        for comp in range(4):
-            basis[comp][slot] = jnp.broadcast_to(upright[:, comp : comp + 1], (BLK, LANES))
+        params[pl.ds(pl.multiple_of(slot * BLK, BLK), BLK), :] = tile[...].T
 
     for slot in range(row_blocks):
-        fill(rank * row_blocks + slot, slot)
+        fill(rank * row_blocks + slot, row_params, slot)
 
     def fill_column(slot, carry):
-        fill(column * col_blocks + slot, row_blocks + slot)
+        fill(column * col_blocks + slot, col_params, slot)
         start = pl.multiple_of(slot * BLK, BLK)
         for row in range(row_blocks):
             piece = density[pl.ds(row * BLK, BLK), pl.ds(start, BLK)]
@@ -108,6 +105,29 @@
     work[filled + 1] = work[jnp.maximum(filled, 1)]
 
 
+def spread(row_params, col_params, basis):
+    row_blocks = row_params.shape[0] // BLK
+
+    def fill(params, slot, target, comp):
+        upright = params[pl.ds(pl.multiple_of(slot * BLK, BLK), BLK), :]
+        basis[target, comp] = jnp.broadcast_to(upright[:, comp : comp + 1], (BLK, LANES))
+
+    for comp in range(4):
+        for row in range(row_blocks):
+            fill(row_params, row, row, comp)
+
+        def fill_columns(step, carry):
+            for unit in range(8):
+                fill(col_params, 8 * step + unit, row_blocks + 8 * step + unit, comp)
+            return carry
+
+        lax.fori_loop(0, col_params.shape[0] // BLK // 8, fill_columns, 0)
+
+
+def side_of(basis, slot):
+    return lambda comp: basis[slot, comp]
+
+
 def total_rows(array):
     return jnp.sum(array, axis=0, keepdims=True)
 
@@ -136,20 +156,18 @@
     return lax.fori_loop(0, lax.shift_right_logical(filled + 1, 1), pair, carry)
 
 
-def density_kernel(work, arrived, at_x, at_y, at_z, rate, forward, backward, out, later):
-    basis = (at_x, at_y, at_z, rate)
-    row_blocks = forward.shape[1]
+def density_kernel(
+    work, arrived, row_params, col_params, forward, backward, out, later, basis
+):
+    row_blocks = row_params.shape[0] // BLK
+    spread(row_params, col_params, basis)
     out[...] = jnp.zeros_like(out)
 
     def partial_sums(entry):
         source, row, block, half = decode(entry)
         point = [arrived[source, pl.ds(half * 4 + comp, 1), :] for comp in range(3)]
-
-        def row_side(comp):
-            return basis[comp][row]
-
-        def col_side(comp):
-            return basis[comp][row_blocks + block]
+        row_side = side_of(basis, row)
+        col_side = side_of(basis, row_blocks + block)
 
         row_values = values_of(row_side, point)
         col_values = values_of(col_side, point)
@@ -266,9 +284,9 @@
         energy_out[batch] = jnp.sum(scale[1, pl.ds(batch * HALVES, HALVES), :])
 
 
-def potential_kernel(work, later, arrived, factors, at_x, at_y, at_z, rate, out):
-    basis = (at_x, at_y, at_z, rate)
-    row_blocks = out.shape[0] // BLK
+def potential_kernel(work, later, arrived, factors, row_params, col_params, out, basis):
+    row_blocks = row_params.shape[0] // BLK
+    spread(row_params, col_params, basis)
     out[...] = jnp.zeros_like(out)
 
     def tile_of(entry, real):
@@ -282,12 +300,8 @@
         def turn(side):
             along_centre = push[0] * side(0) + push[1] * side(1) + push[2] * side(2)
             return (along_point - along_centre) * side(3)
-
-        def row_side(comp):
-            return basis[comp][row]
-
-        def col_side(comp):
-            return basis[comp][row_blocks + block]
+        row_side = side_of(basis, row)
+        col_side = side_of(basis, row_blocks + block)
 
         row_values = values_of(row_side, point)
         col_values = values_of(col_side, point)
@@ -330,9 +344,8 @@
     table = blocks.T
     shape = jax.ShapeDtypeStruct
     messages = shape((sources, 8, LANES), f32)
-    blocks_held = rows // BLK + cols // BLK
     tile_shape = shape((cols // BLK, rows // BLK, BLK, BLK), jnp.bfloat16)
-    spread = shape((blocks_held, BLK, LANES), f32)
+    basis = pltpu.VMEM((rows // BLK + cols // BLK, 4, BLK, LANES), f32)
     listed = shape((sources + 8,), jnp.int32)
 
     outgoing, slots = pl.pallas_call(
@@ -356,11 +369,11 @@
         ]
     )
     arrived = lax.all_to_all(outgoing, "grid", split_axis=0, concat_axis=0, tiled=True)
-    *basis, forward, backward, work = pl.pallas_call(
+    row_params, col_params, forward, backward, work = pl.pallas_call(
         partial(prepare_kernel, group=sources // columns),
-        out_shape=(spread,) * 4 + (tile_shape, tile_shape, listed),
+        out_shape=(shape((rows, 8), f32), shape((cols, 8), f32), tile_shape, tile_shape, listed),
         in_specs=[SMEM, VMEM, VMEM, VMEM],
-        out_specs=(VMEM,) * 6 + (SMEM,),
+        out_specs=(VMEM,) * 4 + (SMEM,),
         scratch_shapes=[pltpu.VMEM((8, LANES), f32)],
         compiler_params=params,
         name="prepare",
@@ -368,11 +381,12 @@
     partials, later = pl.pallas_call(
         density_kernel,
         out_shape=(messages, listed),
-        in_specs=[SMEM] + [VMEM] * 7,
+        in_specs=[SMEM] + [VMEM] * 5,
         out_specs=(VMEM, SMEM),
+        scratch_shapes=[basis],
         compiler_params=params,
         name="density",
-    )(work, arrived, *basis, forward, backward)
+    )(work, arrived, row_params, col_params, forward, backward)
     returned = lax.all_to_all(partials, "grid", split_axis=0, concat_axis=0, tiled=True)
     copies = pl.pallas_call(
         collect_kernel,
@@ -400,11 +414,12 @@
     potential_matrix_xc = pl.pallas_call(
         potential_kernel,
         out_shape=shape((rows, cols), f32),
-        in_specs=[SMEM, SMEM] + [VMEM] * 6,
+        in_specs=[SMEM, SMEM] + [VMEM] * 4,
         out_specs=VMEM,
+        scratch_shapes=[basis],
         compiler_params=params,
         name="potential",
-    )(work, later, arrived, factors, *basis)
+    )(work, later, arrived, factors, row_params, col_params)
     return (potential_matrix_xc, orbital_charge_samples, xc_batch_amounts)
 
 

time: 112 us -> 104 us (0.929); the launches traced: 111 us -> 104 us
  local copies, waits for them, and re-layouts: 10.4 us -> 3.72 us
  blocking collectives: 58 us -> 52.9 us
  waiting for transfers between devices: 0.01 us -> 4.39 us
    unnamed x28 -> x14, local copies, waits for them, and re-layouts: 10.4 us -> 3.72 us
    all_to_all x1, blocking collectives: 24.2 us -> 19.1 us  [local(): lax.all_to_all(partials, 'grid', split_axis=0, concat_axis=0, tiled=True)]
    all_to_all x1, waiting for transfers between devices: 0.01 us -> 4.39 us  [local(): lax.all_to_all(outgoing, 'grid', split_axis=0, concat_axis=0, tiled=True)]
    pallas_call x1, Pallas kernels: 7.44 us -> 4.96 us  [local(): pl.pallas_call(partial(prepare_kernel, group=sources // columns), out_sha...]
    pallas_call x1, Pallas kernels: 8.52 us -> 10.2 us  [local(): pl.pallas_call(potential_kernel, out_shape=shape((rows, cols), f32), in_s...]
    pallas_call x1, Pallas kernels: 7.36 us -> 8.99 us  [local(): pl.pallas_call(density_kernel, out_shape=(messages, listed), in_specs=[SM...]
  transfers between devices with their start and end apart: 1 -> 1, of which waited for: 0 -> 1; matrix products, arithmetic and copies ran while one was open for 0% -> 0% of each run, Pallas kernels for 7% -> 5%
where the time goes in v3:
time: 104 us
  blocking collectives  52.9 us (51%)
  Pallas kernels  27.6 us (27%)
  starting transfers between devices  14.8 us (14%)
  waiting for transfers between devices  4.39 us (4%)
  local copies, waits for them, and re-layouts  3.72 us (4%)
    all_to_all x1, blocking collectives, local(): lax.all_to_all(partials, 'grid', split_axis=0, concat_axis=0, tiled=True)  19.1 us
    all_to_all x1, blocking collectives, local(): lax.all_to_all(sending, 'grid', split_axis=0, concat_axis=0, tiled=True)  19 us
    all_to_all x1, starting transfers between devices, local(): lax.all_to_all(outgoing, 'grid', split_axis=0, concat_axis=0, tiled=True)  14.8 us
    all_to_all x1, blocking collectives, local(): lax.all_to_all(copies, 'col', split_axis=0, concat_axis=0, tiled=True)  14.7 us
    pallas_call x1, Pallas kernels, local(): pl.pallas_call(potential_kernel, out_shape=shape((rows, cols), f32), in_s...  10.2 us
    pallas_call x1, Pallas kernels, local(): pl.pallas_call(density_kernel, out_shape=(messages, listed), in_specs=[SM...  8.99 us
    pallas_call x1, Pallas kernels, local(): pl.pallas_call(partial(prepare_kernel, group=sources // columns), out_sha...  4.96 us
    all_to_all x1, waiting for transfers between devices, local(): lax.all_to_all(outgoing, 'grid', split_axis=0, concat_axis=0, tiled=True)  4.39 us
  transfers between devices with their start and end apart: 1, of which 1 were waited for; matrix products, arithmetic and copies ran while one was open for 0% of the time, Pallas kernels for 5%

profile of v3, /device:TPU:1, one launch (start us, length us, event | category | flops | bytes accessed | tf_op | source)
XLA Modules:
  0.0 104.1 jit_solution(3245858833689244070)
XLA Ops:
  0.6 1.6 %pack.1 = (f32[64,8,128]{2,1,0:T(8,128)}, s32[32]{0:T(128)S(1)}) custom-call(s32[8,256]{1,0:T(8,128)} %bitcast.4, s32[4]{0:T(128)} %counts.1, f32[3,4,256]{2,1,0:T(4,128)} %bitcast.6), custom_call_target="tpu_custom_call" | custom-call | tf_op jit(solution)/shard_map/pack/pallas_call | solution.py:351
  2.2 14.8 %all-to-all-start = ((f32[64,8,128]{2,1,0:T(8,128)}), f32[64,8,128]{2,1,0:T(8,128)S(1)}, u32[]{:S(2)}, u32[]{:S(2)}) async-start(f32[64,8,128]{2,1,0:T(8,128)} %get-tuple-element.16), calls=%async_computation | async-start | bytes 524288 | tf_op jit(solution)/shard_map/all_to_all | solution.py:371
  17.1 0.0 copy-start
  17.1 1.2 %copy-done = bf16[256,2048]{1,0:T(8,128)(2,1)S(1)} copy-done((bf16[256,2048]{1,0:T(8,128)(2,1)S(1)}, bf16[256,2048]{1,0:T(8,128)(2,1)}, u32[]{:S(2)}) %copy-start) | copy-done | bytes 1048600
  18.3 0.0 copy-start.1
  18.3 0.9 copy-done.1
  19.3 0.0 copy-start.2
  19.3 0.8 copy-done.2
  20.1 0.0 copy-start.3
  20.1 0.7 copy-done.3
  20.8 5.0 %prepare.1 = (f32[256,8]{1,0:T(8,128)S(1)}, f32[2048,8]{1,0:T(8,128)S(1)}, bf16[16,2,128,128]{3,2,1,0:T(8,128)(2,1)S(1)}, bf16[16,2,128,128]{3,2,1,0:T(8,128)(2,1)S(1)}, s32[72]{0:T(128)S(1)}) custom-call(s32[8,256]{1,0:T(8,128)S(1)} %bitcast.5, f32[3,16384]{1,0:T(4,128)S(1)} %copy-done.1, f32[128,128]{1,0:T(8,128)S(1)} %bitcast.3, bf16[256,2048]{1,0:T(8,128)(2,1)S(1)} %copy-done), custom_call_target="tpu_custom_call" | custom-call | tf_op jit(solution)/shard_map/prepare/pallas_call | solution.py:372
  25.8 4.4 %all-to-all-done.arrived = f32[64,8,128]{2,1,0:T(8,128)S(1)} async-done(((f32[64,8,128]{2,1,0:T(8,128)}), f32[64,8,128]{2,1,0:T(8,128)S(1)}, u32[]{:S(2)}, u32[]{:S(2)}) %all-to-all-start) | async-done | bytes 262176 | tf_op jit(solution)/shard_map/all_to_all | solution.py:371
  30.2 0.0 copy-start.4
  30.2 0.0 copy-start.5
  30.2 0.0 copy-start.6
  30.2 9.0 %density.3 = (f32[64,8,128]{2,1,0:T(8,128)S(1)}, s32[72]{0:T(128)S(1)}) custom-call(s32[72]{0:T(128)S(1)} %get-tuple-element.15.work, f32[64,8,128]{2,1,0:T(8,128)S(1)} %all-to-all-done.arrived, f32[256,8]{1,0:T(8,128)S(1)} %get-tuple-element.17.row_params, f32[2048,8]{1,0:T(8,128)S(1)} %get-tuple-element.18.col_params, ...), custom_call_target="tpu_custom_call" | custom-call | tf_op jit(solution)/shard_map/density/pallas_call | solution.py:381
  39.2 19.1 %all_to_all.20.arrived = f32[64,8,128]{2,1,0:T(8,128)S(1)} all-to-all(f32[64,8,128]{2,1,0:T(8,128)S(1)} %get-tuple-element.23), channel_id=1, replica_groups=mesh['grid'=64,'col'=8] {'grid'}, dimensions={0} | all-to-all | bytes 524288 | tf_op jit(solution)/shard_map/all_to_all | solution.py:390
  58.3 0.6 collect.1
  58.9 14.7 %all_to_all.21.sums = f32[8,4,8,128]{3,2,1,0:T(8,128)S(1)} all-to-all(f32[8,4,8,128]{3,2,1,0:T(8,128)S(1)} %collect.1), channel_id=1, replica_groups=mesh['grid'=64,'col'=8] {'col'}, dimensions={0} | all-to-all | bytes 262144 | tf_op jit(solution)/shard_map/all_to_all | solution.py:399
  73.6 0.0 copy-done.4
  73.6 0.0 copy-done.5
  73.6 0.0 copy-done.6
  73.6 1.3 %points.1 = (f32[64,8,128]{2,1,0:T(8,128)S(1)}, f32[4,256]{1,0:T(4,128)}, f32[4]{0:T(128)}) custom-call(s32[32]{0:T(128)S(1)} %get-tuple-element.22.slots, s32[4]{0:T(128)S(1)} %copy-done.6, f32[8,4,8,128]{3,2,1,0:T(8,128)S(1)} %all_to_all.21.sums, f32[4,256]{1,0:T(4,128)S(1)} %copy-done.4, f32[4,256]{1,0:T(4,128)S(1)} %copy-done.5), custom_call_target="tpu_custom_call" | custom-call | tf_op jit(solution)/shard_map/points/pallas_call | solution.py:400
  74.9 19.0 %all_to_all.22.factors = f32[64,8,128]{2,1,0:T(8,128)S(1)} all-to-all(f32[64,8,128]{2,1,0:T(8,128)S(1)} %get-tuple-element.24), channel_id=1, replica_groups=mesh['grid'=64,'col'=8] {'grid'}, dimensions={0} | all-to-all | bytes 524288 | tf_op jit(solution)/shard_map/all_to_all | solution.py:413
  93.9 10.2 %potential.1 = f32[256,2048]{1,0:T(8,128)} custom-call(s32[72]{0:T(128)S(1)} %get-tuple-element.15.work, s32[72]{0:T(128)S(1)} %get-tuple-element.21.later, f32[64,8,128]{2,1,0:T(8,128)S(1)} %all-to-all-done.arrived, f32[64,8,128]{2,1,0:T(8,128)S(1)} %all_to_all.22.factors, f32[256,8]{1,0:T(8,128)S(1)} %get-tuple-element.17.row_params, ...), custom_call_target="tpu_custom_call" | custom-call | tf_op jit(solution)/shard_map/potential/pallas_call | solution.py:414
Async XLA Ops:
  2.2 27.9 %all-to-all-start = ((f32[64,8,128]{2,1,0:T(8,128)}), f32[64,8,128]{2,1,0:T(8,128)S(1)}, u32[]{:S(2)}, u32[]{:S(2)}) async-start(f32[64,8,128]{2,1,0:T(8,128)} %get-tuple-element.16), calls=%async_computation | async-start | bytes 524288 | tf_op jit(solution)/shard_map/all_to_all | solution.py:371
  17.1 1.2 %copy-start = (bf16[256,2048]{1,0:T(8,128)(2,1)S(1)}, bf16[256,2048]{1,0:T(8,128)(2,1)}, u32[]{:S(2)}) copy-start(bf16[256,2048]{1,0:T(8,128)(2,1)} %density.2) | copy-start | bytes 3145732
  18.3 0.9 copy-start.1
  19.3 0.8 copy-start.2
  20.1 0.7 copy-start.3
  30.2 43.4 %copy-start.4 = (f32[4,256]{1,0:T(4,128)S(1)}, f32[4,256]{1,0:T(4,128)}, u32[]{:S(2)}) copy-start(f32[4,256]{1,0:T(4,128)} %weights.1) | copy-start | bytes 12292
  30.2 43.4 %copy-start.5 = (f32[4,256]{1,0:T(4,128)S(1)}, f32[4,256]{1,0:T(4,128)}, u32[]{:S(2)}) copy-start(f32[4,256]{1,0:T(4,128)} %core.1) | copy-start | bytes 12292
  30.2 43.4 %copy-start.6 = (s32[4]{0:T(128)S(1)}, s32[4]{0:T(128)}, u32[]{:S(2)}) copy-start(s32[4]{0:T(128)} %counts.1) | copy-start | bytes 52

commit v4 on v3

--- a/solution.py
+++ b/solution.py
@@ -23,6 +23,8 @@
 VMEM = pl.BlockSpec(memory_space=pltpu.VMEM)
 
 
+PIECES = 3
+GROUP = 4
 LOG2E = math.log2(math.e)
 SLOPE = 2.0 * math.log(2.0)
 HBM = pl.BlockSpec(memory_space=pltpu.HBM)
@@ -58,7 +60,7 @@
             out[slot] = tile
 
 
-def prepare_kernel(table, centres, exponents, density, row_params, col_params, forward, backward, work, tile, *, group):
+def prepare_kernel(table, centres, exponents, density, pieces, forward, backward, work, tile, *, group):
     rank = lax.axis_index("grid")
     column = lax.axis_index("col")
     own = rank // group
@@ -67,17 +69,22 @@
     sources = table.shape[1] // NB
     tile[...] = jnp.zeros_like(tile)
 
-    def fill(block, params, slot):
+    def fill(block, slot):
         start = pl.multiple_of(block * BLK, BLK)
         tile[pl.ds(0, 3), :] = centres[:, pl.ds(start, BLK)]
         tile[pl.ds(3, 1), :] = exponents[pl.ds(block, 1), :] * (-LOG2E)
-        params[pl.ds(pl.multiple_of(slot * BLK, BLK), BLK), :] = tile[...].T
+        rest = tile[pl.ds(0, 8), :]
+        for index in range(PIECES):
+            piece = rest.astype(jnp.bfloat16).astype(jnp.float32)
+            tile[pl.ds((index + 1) * 8, 8), :] = piece
+            rest = rest - piece
+        pieces[slot] = tile[pl.ds(8, BLK), :].astype(jnp.bfloat16).T
 
     for slot in range(row_blocks):
-        fill(rank * row_blocks + slot, row_params, slot)
+        fill(rank * row_blocks + slot, slot)
 
     def fill_column(slot, carry):
-        fill(column * col_blocks + slot, col_params, slot)
+        fill(column * col_blocks + slot, row_blocks + slot)
         start = pl.multiple_of(slot * BLK, BLK)
         for row in range(row_blocks):
             piece = density[pl.ds(row * BLK, BLK), pl.ds(start, BLK)]
@@ -101,27 +108,22 @@
         return filled
 
     filled = lax.fori_loop(0, sources // 4, list_sources, jnp.int32(0))
-    work[0] = filled
-    work[filled + 1] = work[jnp.maximum(filled, 1)]
-
-
-def spread(row_params, col_params, basis):
-    row_blocks = row_params.shape[0] // BLK
-
-    def fill(params, slot, target, comp):
-        upright = params[pl.ds(pl.multiple_of(slot * BLK, BLK), BLK), :]
-        basis[target, comp] = jnp.broadcast_to(upright[:, comp : comp + 1], (BLK, LANES))
-
-    for comp in range(4):
-        for row in range(row_blocks):
-            fill(row_params, row, row, comp)
-
-        def fill_columns(step, carry):
-            for unit in range(8):
-                fill(col_params, 8 * step + unit, row_blocks + 8 * step + unit, comp)
-            return carry
-
-        lax.fori_loop(0, col_params.shape[0] // BLK // 8, fill_columns, 0)
+    close_list(work, filled)
+
+
+def spread(pieces, basis):
+    index = lax.broadcasted_iota(jnp.int32, (BLK, 4 * LANES), 0)
+    lane = lax.broadcasted_iota(jnp.int32, (BLK, 4 * LANES), 1)
+    picked = jnp.logical_and(index < 8 * PIECES, (index & 7) == lax.shift_right_logical(lane, 7))
+    chooser = jnp.where(picked, 1.0, 0.0).astype(jnp.bfloat16)
+
+    def fill(slot, carry):
+        wide = jnp.dot(pieces[slot], chooser, preferred_element_type=jnp.float32)
+        for comp in range(4):
+            basis[slot, comp] = wide[:, comp * LANES : (comp + 1) * LANES]
+        return carry
+
+    lax.fori_loop(0, pieces.shape[0], fill, 0, unroll=2)
 
 
 def side_of(basis, slot):
@@ -146,21 +148,29 @@
     return jnp.exp2(distance * side(3))
 
 
-def over_pairs(work, handle, carry):
+def close_list(work, filled):
+    work[0] = filled
+    for unit in range(1, GROUP):
+        work[filled + unit] = work[jnp.maximum(filled, 1)]
+
+
+def over_groups(work, handle, carry):
     filled = work[0]
 
-    def pair(step, carry):
-        entries = [(work[2 * step + unit + 1], 2 * step + unit < filled) for unit in range(2)]
+    def group(step, carry):
+        entries = [
+            (work[GROUP * step + unit + 1], GROUP * step + unit < filled) for unit in range(GROUP)
+        ]
         return handle(entries, carry)
 
-    return lax.fori_loop(0, lax.shift_right_logical(filled + 1, 1), pair, carry)
+    return lax.fori_loop(0, (filled + GROUP - 1) // GROUP, group, carry)
 
 
 def density_kernel(
-    work, arrived, row_params, col_params, forward, backward, out, later, basis
+    work, arrived, pieces, forward, backward, out, later, basis
 ):
-    row_blocks = row_params.shape[0] // BLK
-    spread(row_params, col_params, basis)
+    row_blocks = forward.shape[1]
+    spread(pieces, basis)
     out[...] = jnp.zeros_like(out)
 
     def partial_sums(entry):
@@ -201,10 +211,9 @@
                 out[source, pl.ds(half * 4 + comp, 1), :] = sums[comp]
         return carry
 
-    filled = over_pairs(work, first_halves, jnp.int32(0))
-    later[0] = filled
-    later[filled + 1] = later[jnp.maximum(filled, 1)]
-    over_pairs(later, halves, 0)
+    filled = over_groups(work, first_halves, jnp.int32(0))
+    close_list(later, filled)
+    over_groups(later, halves, 0)
 
 
 def collect_kernel(slots, arrived, out):
@@ -284,9 +293,9 @@
         energy_out[batch] = jnp.sum(scale[1, pl.ds(batch * HALVES, HALVES), :])
 
 
-def potential_kernel(work, later, arrived, factors, row_params, col_params, out, basis):
-    row_blocks = row_params.shape[0] // BLK
-    spread(row_params, col_params, basis)
+def potential_kernel(work, later, arrived, factors, pieces, out, basis):
+    row_blocks = out.shape[0] // BLK
+    spread(pieces, basis)
     out[...] = jnp.zeros_like(out)
 
     def tile_of(entry, real):
@@ -330,8 +339,8 @@
             out[place] = out[place] + product
         return carry
 
-    over_pairs(work, handle, 0)
-    over_pairs(later, handle, 0)
+    over_groups(work, handle, 0)
+    over_groups(later, handle, 0)
 
 
 def local(density, centres, exponents, coords, weights, core_density, counts, blocks):
@@ -369,24 +378,29 @@
         ]
     )
     arrived = lax.all_to_all(outgoing, "grid", split_axis=0, concat_axis=0, tiled=True)
-    row_params, col_params, forward, backward, work = pl.pallas_call(
+    pieces, forward, backward, work = pl.pallas_call(
         partial(prepare_kernel, group=sources // columns),
-        out_shape=(shape((rows, 8), f32), shape((cols, 8), f32), tile_shape, tile_shape, listed),
+        out_shape=(
+            shape((rows // BLK + cols // BLK, BLK, BLK), jnp.bfloat16),
+            tile_shape,
+            tile_shape,
+            listed,
+        ),
         in_specs=[SMEM, VMEM, VMEM, VMEM],
-        out_specs=(VMEM,) * 4 + (SMEM,),
-        scratch_shapes=[pltpu.VMEM((8, LANES), f32)],
+        out_specs=(VMEM,) * 3 + (SMEM,),
+        scratch_shapes=[pltpu.VMEM((8 + BLK, LANES), f32)],
         compiler_params=params,
         name="prepare",
     )(table, centres, exponents.reshape(-1, LANES), density)
     partials, later = pl.pallas_call(
         density_kernel,
         out_shape=(messages, listed),
-        in_specs=[SMEM] + [VMEM] * 5,
+        in_specs=[SMEM] + [VMEM] * 4,
         out_specs=(VMEM, SMEM),
         scratch_shapes=[basis],
         compiler_params=params,
         name="density",
-    )(work, arrived, row_params, col_params, forward, backward)
+    )(work, arrived, pieces, forward, backward)
     returned = lax.all_to_all(partials, "grid", split_axis=0, concat_axis=0, tiled=True)
     copies = pl.pallas_call(
         collect_kernel,
@@ -414,12 +428,12 @@
     potential_matrix_xc = pl.pallas_call(
         potential_kernel,
         out_shape=shape((rows, cols), f32),
-        in_specs=[SMEM, SMEM] + [VMEM] * 4,
+        in_specs=[SMEM, SMEM] + [VMEM] * 3,
         out_specs=VMEM,
         scratch_shapes=[basis],
         compiler_params=params,
         name="potential",
-    )(work, later, arrived, factors, row_params, col_params)
+    )(work, later, arrived, factors, pieces)
     return (potential_matrix_xc, orbital_charge_samples, xc_batch_amounts)
 
 

time: 104 us -> 101 us (0.971)
  Pallas kernels: 27.6 us -> 22.9 us
    pallas_call x1, Pallas kernels: 8.99 us -> 6.82 us  [local(): pl.pallas_call(density_kernel, out_shape=(messages, listed), in_specs=[SM...]
    pallas_call x1, Pallas kernels: 10.2 us -> 8.1 us  [local(): pl.pallas_call(potential_kernel, out_shape=shape((rows, cols), f32), in_s...]
where the time goes in v4:
time: 101 us; the launch traced here: 100 us
  blocking collectives  53.4 us (53%)
  Pallas kernels  22.9 us (23%)
  starting transfers between devices  14.8 us (15%)
  waiting for transfers between devices  4.76 us (5%)
  local copies, waits for them, and re-layouts  3.72 us (4%)
    all_to_all x1, blocking collectives, local(): lax.all_to_all(partials, 'grid', split_axis=0, concat_axis=0, tiled=True)  19.7 us
    all_to_all x1, blocking collectives, local(): lax.all_to_all(sending, 'grid', split_axis=0, concat_axis=0, tiled=True)  19 us
    all_to_all x1, starting transfers between devices, local(): lax.all_to_all(outgoing, 'grid', split_axis=0, concat_axis=0, tiled=True)  14.8 us
    all_to_all x1, blocking collectives, local(): lax.all_to_all(copies, 'col', split_axis=0, concat_axis=0, tiled=True)  14.7 us
    pallas_call x1, Pallas kernels, local(): pl.pallas_call(potential_kernel, out_shape=shape((rows, cols), f32), in_s...  8.1 us
    pallas_call x1, Pallas kernels, local(): pl.pallas_call(density_kernel, out_shape=(messages, listed), in_specs=[SM...  6.82 us
    all_to_all x1, waiting for transfers between devices, local(): lax.all_to_all(outgoing, 'grid', split_axis=0, concat_axis=0, tiled=True)  4.76 us
    pallas_call x1, Pallas kernels, local(): pl.pallas_call(partial(prepare_kernel, group=sources // columns), out_sha...  4.55 us
  transfers between devices with their start and end apart: 1, of which 1 were waited for; matrix products, arithmetic and copies ran while one was open for 0% of the time, Pallas kernels for 5%

profile of v4, /device:TPU:1, one launch (start us, length us, event | category | flops | bytes accessed | tf_op | source)
XLA Modules:
  0.0 100.4 jit_solution(17849040088198663673)
XLA Ops:
  0.6 1.6 %pack.1 = (f32[64,8,128]{2,1,0:T(8,128)}, s32[32]{0:T(128)S(1)}) custom-call(s32[8,256]{1,0:T(8,128)} %bitcast.4, s32[4]{0:T(128)} %counts.1, f32[3,4,256]{2,1,0:T(4,128)} %bitcast.6), custom_call_target="tpu_custom_call" | custom-call | tf_op jit(solution)/shard_map/pack/pallas_call | solution.py:360
  2.2 14.8 %all-to-all-start = ((f32[64,8,128]{2,1,0:T(8,128)}), f32[64,8,128]{2,1,0:T(8,128)S(1)}, u32[]{:S(2)}, u32[]{:S(2)}) async-start(f32[64,8,128]{2,1,0:T(8,128)} %get-tuple-element.15), calls=%async_computation | async-start | bytes 524288 | tf_op jit(solution)/shard_map/all_to_all | solution.py:380
  17.1 0.0 copy-start
  17.1 1.2 %copy-done = bf16[256,2048]{1,0:T(8,128)(2,1)S(1)} copy-done((bf16[256,2048]{1,0:T(8,128)(2,1)S(1)}, bf16[256,2048]{1,0:T(8,128)(2,1)}, u32[]{:S(2)}) %copy-start) | copy-done | bytes 1048600
  18.3 0.0 copy-start.1
  18.3 0.9 copy-done.1
  19.3 0.0 copy-start.2
  19.3 0.8 copy-done.2
  20.1 0.0 copy-start.3
  20.1 0.7 copy-done.3
  20.8 4.6 %prepare.1 = (bf16[18,128,128]{2,1,0:T(8,128)(2,1)S(1)}, bf16[16,2,128,128]{3,2,1,0:T(8,128)(2,1)S(1)}, bf16[16,2,128,128]{3,2,1,0:T(8,128)(2,1)S(1)}, s32[72]{0:T(128)S(1)}) custom-call(s32[8,256]{1,0:T(8,128)S(1)} %bitcast.5, f32[3,16384]{1,0:T(4,128)S(1)} %copy-done.1, f32[128,128]{1,0:T(8,128)S(1)} %bitcast.3, bf16[256,2048]{1,0:T(8,128)(2,1)S(1)} %copy-done), custom_call_target="tpu_custom_call" | custom-call | tf_op jit(solution)/shard_map/prepare/pallas_call | solution.py:381
  25.4 0.0 copy-start.4
  25.4 0.0 copy-start.5
  25.4 0.0 copy-start.6
  25.4 4.8 %all-to-all-done.arrived = f32[64,8,128]{2,1,0:T(8,128)S(1)} async-done(((f32[64,8,128]{2,1,0:T(8,128)}), f32[64,8,128]{2,1,0:T(8,128)S(1)}, u32[]{:S(2)}, u32[]{:S(2)}) %all-to-all-start) | async-done | bytes 262176 | tf_op jit(solution)/shard_map/all_to_all | solution.py:380
  30.2 6.8 %density.3 = (f32[64,8,128]{2,1,0:T(8,128)S(1)}, s32[72]{0:T(128)S(1)}) custom-call(s32[72]{0:T(128)S(1)} %get-tuple-element.14.work, f32[64,8,128]{2,1,0:T(8,128)S(1)} %all-to-all-done.arrived, bf16[18,128,128]{2,1,0:T(8,128)(2,1)S(1)} %get-tuple-element.16.pieces, bf16[16,2,128,128]{3,2,1,0:T(8,128)(2,1)S(1)} %get-tuple-element.17.forward, ...), custom_call_target="tpu_custom_call" | custom-call | tf_op jit(solution)/shard_map/density/pallas_call | solution.py:395
  37.0 19.7 %all_to_all.20.arrived = f32[64,8,128]{2,1,0:T(8,128)S(1)} all-to-all(f32[64,8,128]{2,1,0:T(8,128)S(1)} %get-tuple-element.21), channel_id=1, replica_groups=mesh['grid'=64,'col'=8] {'grid'}, dimensions={0} | all-to-all | bytes 524288 | tf_op jit(solution)/shard_map/all_to_all | solution.py:404
  56.7 0.6 collect.1
  57.3 14.7 %all_to_all.21.sums = f32[8,4,8,128]{3,2,1,0:T(8,128)S(1)} all-to-all(f32[8,4,8,128]{3,2,1,0:T(8,128)S(1)} %collect.1), channel_id=1, replica_groups=mesh['grid'=64,'col'=8] {'col'}, dimensions={0} | all-to-all | bytes 262144 | tf_op jit(solution)/shard_map/all_to_all | solution.py:413
  72.0 0.0 copy-done.4
  72.0 0.0 copy-done.5
  72.0 0.0 copy-done.6
  72.0 1.3 %points.1 = (f32[64,8,128]{2,1,0:T(8,128)S(1)}, f32[4,256]{1,0:T(4,128)}, f32[4]{0:T(128)}) custom-call(s32[32]{0:T(128)S(1)} %get-tuple-element.20.slots, s32[4]{0:T(128)S(1)} %copy-done.6, f32[8,4,8,128]{3,2,1,0:T(8,128)S(1)} %all_to_all.21.sums, f32[4,256]{1,0:T(4,128)S(1)} %copy-done.4, f32[4,256]{1,0:T(4,128)S(1)} %copy-done.5), custom_call_target="tpu_custom_call" | custom-call | tf_op jit(solution)/shard_map/points/pallas_call | solution.py:414
  73.2 19.0 %all_to_all.22.factors = f32[64,8,128]{2,1,0:T(8,128)S(1)} all-to-all(f32[64,8,128]{2,1,0:T(8,128)S(1)} %get-tuple-element.22), channel_id=1, replica_groups=mesh['grid'=64,'col'=8] {'grid'}, dimensions={0} | all-to-all | bytes 524288 | tf_op jit(solution)/shard_map/all_to_all | solution.py:427
  92.3 8.1 %potential.1 = f32[256,2048]{1,0:T(8,128)} custom-call(s32[72]{0:T(128)S(1)} %get-tuple-element.14.work, s32[72]{0:T(128)S(1)} %get-tuple-element.19.later, f32[64,8,128]{2,1,0:T(8,128)S(1)} %all-to-all-done.arrived, f32[64,8,128]{2,1,0:T(8,128)S(1)} %all_to_all.22.factors, bf16[18,128,128]{2,1,0:T(8,128)(2,1)S(1)} %get-tuple-element.16.pieces), custom_call_target="tpu_custom_call" | custom-call | tf_op jit(solution)/shard_map/potential/pallas_call | solution.py:428
Async XLA Ops:
  2.2 27.9 %all-to-all-start = ((f32[64,8,128]{2,1,0:T(8,128)}), f32[64,8,128]{2,1,0:T(8,128)S(1)}, u32[]{:S(2)}, u32[]{:S(2)}) async-start(f32[64,8,128]{2,1,0:T(8,128)} %get-tuple-element.15), calls=%async_computation | async-start | bytes 524288 | tf_op jit(solution)/shard_map/all_to_all | solution.py:380
  17.1 1.2 %copy-start = (bf16[256,2048]{1,0:T(8,128)(2,1)S(1)}, bf16[256,2048]{1,0:T(8,128)(2,1)}, u32[]{:S(2)}) copy-start(bf16[256,2048]{1,0:T(8,128)(2,1)} %density.2) | copy-start | bytes 3145732
  18.3 0.9 copy-start.1
  19.3 0.8 copy-start.2
  20.1 0.7 copy-start.3
  25.4 46.6 %copy-start.4 = (f32[4,256]{1,0:T(4,128)S(1)}, f32[4,256]{1,0:T(4,128)}, u32[]{:S(2)}) copy-start(f32[4,256]{1,0:T(4,128)} %weights.1) | copy-start | bytes 12292
  25.4 46.6 %copy-start.5 = (f32[4,256]{1,0:T(4,128)S(1)}, f32[4,256]{1,0:T(4,128)}, u32[]{:S(2)}) copy-start(f32[4,256]{1,0:T(4,128)} %core.1) | copy-start | bytes 12292
  25.4 46.6 %copy-start.6 = (s32[4]{0:T(128)S(1)}, s32[4]{0:T(128)}, u32[]{:S(2)}) copy-start(s32[4]{0:T(128)} %counts.1) | copy-start | bytes 52

commit v5 on v4

v5 whole, which is shorter than its diff:
```python
from functools import partial
import math

import jax
import jax.numpy as jnp
from jax import lax
from jax.experimental import pallas as pl
from jax.experimental.pallas import tpu as pltpu
from jax.sharding import PartitionSpec as P

BLK = 128
NB = 4
LANES = 128
HALVES = 2

kappa_pbe = 0.804
mu_coef = 0.2195
slater = -0.7385587663820224
grad_scale = 4.0 * (3.0 * math.pi**2) ** (2.0 / 3.0)
soft_square = 0.25

SMEM = pl.BlockSpec(memory_space=pltpu.SMEM)
VMEM = pl.BlockSpec(memory_space=pltpu.VMEM)


PIECES = 3
GROUP = 4
REAL = 1 << 16
FAR = 64.0
LOG2E = math.log2(math.e)
SLOPE = 2.0 * math.log(2.0)
HBM = pl.BlockSpec(memory_space=pltpu.HBM)


def start_all(pairs, sems):
    copies = [
        pltpu.make_async_copy(source, target, sems.at[index])
        for index, (source, target) in enumerate(pairs)
    ]
    for copy in copies:
        copy.start()
    return copies


def pack_kernel(table_hbm, counts_hbm, coords_hbm, out, slots, table, counts, coords, sems):
    copies = start_all([(table_hbm, table), (counts_hbm, counts), (coords_hbm, coords)], sems)
    first = lax.axis_index("grid") * NB
    columns = table.shape[0]
    points = coords.shape[2]
    lane = lax.broadcasted_iota(jnp.int32, (1, points), 1)
    for copy in copies:
        copy.wait()
    for batch in range(NB):
        live = lane < counts[batch]
        message = jnp.concatenate(
            [jnp.where(live, coords[comp, pl.ds(batch, 1), :], FAR) for comp in range(3)], axis=1
        )
        for column in range(columns):
            slot = lax.shift_right_logical(table[column, first + batch], 1)
            slots[column * NB + batch] = slot
            out[slot] = message


def prepare_kernel(*refs, group):
    hbm, (pieces, forward, backward, scale, work) = refs[:7], refs[7:12]
    table, counts, centres, exponents, weights, core, density = refs[12:19]
    tile, sems = refs[19:]
    copies = start_all(list(zip(hbm, refs[12:19])), sems)
    rank = lax.axis_index("grid")
    column = lax.axis_index("col")
    own = rank // group
    row_blocks = density.shape[0] // BLK
    col_blocks = density.shape[1] // BLK
    sources = table.shape[1] // NB
    for copy in copies[:2]:
        copy.wait()

    def list_sources(step, filled):
        for unit in range(4):
            source = step * 4 + unit
            code = jnp.int32(0)
            for batch in range(NB):
                part = table[own, source * NB + batch] ^ (2 * rank)
                code = jnp.where(part < 2, 8 + 2 * batch + part, code)
            choice = lax.shift_right_logical(code, 1) & 3
            target = table[column, source * NB + choice] - column * col_blocks
            work[filled + 1] = source * 64 + (code & 1) * 32 + target * 2
            filled = filled + lax.shift_right_logical(code, 3)
        return filled

    filled = lax.fori_loop(0, sources // 4, list_sources, jnp.int32(0))
    close_list(work, filled)

    for copy in copies[4:6]:
        copy.wait()
    lane = lax.broadcasted_iota(jnp.int32, (1, LANES), 1)
    for batch in range(NB):
        for half in range(HALVES):
            place = pl.ds(batch * HALVES + half, 1)
            part = (pl.ds(batch, 1), pl.ds(half * LANES, LANES))
            live = jnp.where(lane + half * LANES < counts[batch], 1.0, 0.0).astype(jnp.float32)
            scale[0, place, :] = live
            scale[1, place, :] = weights[part] * live
            scale[2, place, :] = core[part]

    tile[...] = jnp.zeros_like(tile)

    def fill(block, slot):
        start = pl.multiple_of(block * BLK, BLK)
        tile[pl.ds(0, 3), :] = centres[:, pl.ds(start, BLK)]
        tile[pl.ds(3, 1), :] = exponents[pl.ds(block, 1), :] * (-LOG2E)
        rest = tile[pl.ds(0, 8), :]
        for index in range(PIECES):
            piece = rest.astype(jnp.bfloat16).astype(jnp.float32)
            tile[pl.ds((index + 1) * 8, 8), :] = piece
            rest = rest - piece
        pieces[slot] = tile[pl.ds(8, BLK), :].astype(jnp.bfloat16).T

    for copy in copies[2:4]:
        copy.wait()
    for slot in range(row_blocks):
        fill(rank * row_blocks + slot, slot)

    def fill_column(slot, carry):
        fill(column * col_blocks + slot, row_blocks + slot)
        start = pl.multiple_of(slot * BLK, BLK)
        for row in range(row_blocks):
            piece = density[pl.ds(row * BLK, BLK), pl.ds(start, BLK)]
            forward[slot, row] = piece
            backward[slot, row] = piece.T
        return carry

    copies[6].wait()
    lax.fori_loop(0, col_blocks, fill_column, 0)


def spread(pieces, basis):
    index = lax.broadcasted_iota(jnp.int32, (BLK, 4 * LANES), 0)
    lane = lax.broadcasted_iota(jnp.int32, (BLK, 4 * LANES), 1)
    picked = jnp.logical_and(index < 8 * PIECES, (index & 7) == lax.shift_right_logical(lane, 7))
    chooser = jnp.where(picked, 1.0, 0.0).astype(jnp.bfloat16)

    def fill(slot, carry):
        wide = jnp.dot(pieces[slot], chooser, preferred_element_type=jnp.float32)
        for comp in range(4):
            basis[slot, comp] = wide[:, comp * LANES : (comp + 1) * LANES]
        return carry

    lax.fori_loop(0, pieces.shape[0], fill, 0, unroll=2)


def side_of(basis, slot):
    return lambda comp: basis[slot, comp]


def total_rows(array):
    return jnp.sum(array, axis=0, keepdims=True)


def decode(entry):
    half = entry & 1
    block = lax.shift_right_logical(entry, 1) & 15
    row = lax.shift_right_logical(entry, 5) & 1
    source = lax.shift_right_logical(entry, 6) & 1023
    return source, row, block, half


def point_of(arrived, source, half):
    points = arrived.shape[2] // 3
    return [
        arrived[source, :, pl.ds(pl.multiple_of(comp * points + half * LANES, LANES), LANES)]
        for comp in range(3)
    ]


def values_of(side, point):
    offset = [point[comp] - side(comp) for comp in range(3)]
    distance = offset[0] * offset[0] + offset[1] * offset[1] + offset[2] * offset[2]
    return jnp.exp2(distance * side(3))


def close_list(work, filled):
    work[0] = filled
    for unit in range(1, GROUP):
        work[filled + unit] = work[jnp.maximum(filled, 1)]


def groups_of(work):
    return (work[0] + GROUP - 1) // GROUP


def density_kernel(
    work, arrived, pieces, forward, backward, out, done, kept, later, basis, hold, sems
):
    row_blocks = forward.shape[1]
    spread(pieces, basis)
    out[...] = jnp.zeros_like(out)

    def partial_sums(entry):
        source, row, block, half = decode(entry)
        point = point_of(arrived, source, half)
        row_side = side_of(basis, row)
        col_side = side_of(basis, row_blocks + block)

        row_values = values_of(row_side, point)
        col_values = values_of(col_side, point)
        right = jnp.dot(
            backward[block, row], row_values.astype(jnp.bfloat16), preferred_element_type=jnp.float32
        )
        left = jnp.dot(
            forward[block, row], col_values.astype(jnp.bfloat16), preferred_element_type=jnp.float32
        )
        col_product = col_values * right
        col_slope = col_product * col_side(3)
        row_slope = row_values * left * row_side(3)
        slope = total_rows(row_slope + col_slope)
        sums = [total_rows(col_product)]
        for comp in range(3):
            moment = total_rows(row_slope * row_side(comp) + col_slope * col_side(comp))
            sums.append(SLOPE * (point[comp] * slope - moment))
        return source, half, sums, row_values, col_values

    def write_back(index):
        slot = index & 1
        return pltpu.make_async_copy(hold.at[slot], kept.at[index], sems.at[slot])

    def group(work, step, index):
        @pl.when(index >= 2)
        def _():
            write_back(index - 2).wait()

        entries = [work[GROUP * step + unit + 1] for unit in range(GROUP)]
        results = [partial_sums(entry) for entry in entries]
        for unit, (source, half, sums, row_values, col_values) in enumerate(results):
            for comp in range(4):
                out[source, pl.ds(half * 4 + comp, 1), :] = sums[comp]
            hold[index & 1, unit, 0] = row_values
            hold[index & 1, unit, 1] = col_values
            real = jnp.where(GROUP * step + unit < work[0], REAL, 0)
            done[GROUP * index + unit + 1] = entries[unit] + real
        write_back(index).start()

    def first_halves(step, filled):
        for unit in range(GROUP):
            entry = work[GROUP * step + unit + 1]
            beyond = point_of(arrived, decode(entry)[0], 1)[0][0, 0]
            later[filled + 1] = entry + 1
            real = jnp.logical_and(beyond < FAR, GROUP * step + unit < work[0])
            filled = filled + jnp.where(real, 1, 0)
        group(work, step, step)
        return filled

    firsts = groups_of(work)
    filled = lax.fori_loop(0, firsts, first_halves, jnp.int32(0))
    close_list(later, filled)

    def second_halves(step, carry):
        group(later, step, firsts + step)
        return carry

    total = firsts + groups_of(later)
    lax.fori_loop(0, groups_of(later), second_halves, 0)
    done[0] = total
    for back in (2, 1):

        @pl.when(total >= back)
        def _():
            write_back(total - back).wait()


def collect_kernel(slots, arrived, out):
    columns = slots.shape[0] // NB
    for batch in range(NB):
        total = arrived[slots[batch]]
        for column in range(1, columns):
            total = total + arrived[slots[column * NB + batch]]
        for copy in range(out.shape[0]):
            out[copy, batch] = total


def point_kernel(
    slots, sums, scale, out, charge_out, energy_out, summed, tiles, results_at
):
    columns = slots.shape[0] // NB
    for batch in range(NB):
        total = sums[0, batch]
        for column in range(1, sums.shape[0]):
            total = total + sums[column, batch]
        summed[pl.ds(batch * 8, 8), :] = total
    live = scale[0]
    point_scale = scale[1]
    count_rows = NB * HALVES
    valence = live * summed[pl.ds(0, count_rows, stride=4), :]
    gradient = [live * summed[pl.ds(comp + 1, count_rows, stride=4), :] for comp in range(3)]
    grad_square = (
        gradient[0] * gradient[0] + gradient[1] * gradient[1] + gradient[2] * gradient[2]
    )
    total = valence + scale[2]
    root = jnp.sqrt(total * total + soft_square)
    regular = 0.5 * (total + root)
    third = jnp.exp(jnp.log(regular) * (1.0 / 3.0))
    four_thirds = regular * third
    scaled = grad_scale * four_thirds * four_thirds
    weighted = mu_coef * grad_square
    inverse = 1.0 / (kappa_pbe * scaled + weighted)
    fraction = scaled * inverse
    enhance = 1.0 + kappa_pbe - kappa_pbe * kappa_pbe * fraction
    energy = slater * four_thirds * enhance
    square = kappa_pbe * kappa_pbe * mu_coef
    deriv_sigma = slater * four_thirds * (square * fraction * inverse)
    enhance_slope = (
        -(kappa_pbe * kappa_pbe)
        * (weighted * inverse)
        * inverse
        * (grad_scale * (8.0 / 3.0) * four_thirds * third)
    )
    deriv_regular = slater * ((4.0 / 3.0) * third * enhance + four_thirds * enhance_slope)
    deriv_density = deriv_regular * (0.5 * (1.0 + total / root))
    fweight = point_scale * deriv_density
    factor = 2.0 * point_scale * deriv_sigma
    results = [fweight] + [factor * gradient[comp] for comp in range(3)]
    for comp in range(4):
        tiles[pl.ds(comp, count_rows, stride=4), :] = results[comp]
    for batch in range(NB):
        tile = tiles[pl.ds(batch * 8, 8), :]
        for column in range(columns):
            out[slots[column * NB + batch]] = tile
    results_at[0] = valence
    results_at[1] = point_scale * energy
    for batch in range(NB):
        for half in range(HALVES):
            charge_out[pl.ds(batch, 1), pl.ds(half * LANES, LANES)] = results_at[
                0, pl.ds(batch * HALVES + half, 1), :
            ]
        energy_out[batch] = jnp.sum(results_at[1, pl.ds(batch * HALVES, HALVES), :])


def potential_kernel(done, arrived, factors, pieces, kept, out, basis, held, sems):
    row_blocks = out.shape[0] // BLK
    total = done[0]

    def fetch(index):
        slot = index & 1
        return pltpu.make_async_copy(kept.at[index], held.at[slot], sems.at[slot])

    @pl.when(total > 0)
    def _():
        fetch(0).start()

    spread(pieces, basis)
    out[...] = jnp.zeros_like(out)

    def tile_of(entry, row_values, col_values):
        source, row, block, half = decode(entry)
        keep = jnp.where(entry >= REAL, 1.0, 0.0).astype(jnp.float32)
        point = point_of(arrived, source, half)
        factor = [factors[source, pl.ds(half * 4 + comp, 1), :] * keep for comp in range(4)]
        push = [SLOPE * factor[comp + 1] for comp in range(3)]
        along_point = push[0] * point[0] + push[1] * point[1] + push[2] * point[2]

        def turn(side):
            along_centre = push[0] * side(0) + push[1] * side(1) + push[2] * side(2)
            return (along_point - along_centre) * side(3)
        row_side = side_of(basis, row)
        col_side = side_of(basis, row_blocks + block)

        row_across = row_values * turn(row_side)
        along = col_values * (factor[0] + turn(col_side))
        left_side = jnp.concatenate(
            [row_values.astype(jnp.bfloat16), row_across.astype(jnp.bfloat16)], axis=1
        )
        right_side = jnp.concatenate(
            [along.astype(jnp.bfloat16), col_values.astype(jnp.bfloat16)], axis=1
        )
        product = lax.dot_general(
            left_side,
            right_side,
            (((1,), (1,)), ((), ())),
            preferred_element_type=jnp.float32,
        )
        row_start = pl.multiple_of(row * BLK, BLK)
        col_start = pl.multiple_of(block * BLK, BLK)
        return row_start, col_start, product

    def group(index, carry):
        @pl.when(index + 1 < total)
        def _():
            fetch(index + 1).start()

        fetch(index).wait()
        results = [
            tile_of(
                done[GROUP * index + unit + 1], held[index & 1, unit, 0], held[index & 1, unit, 1]
            )
            for unit in range(GROUP)
        ]
        for row_start, col_start, product in results:
            place = (pl.ds(row_start, BLK), pl.ds(col_start, BLK))
            out[place] = out[place] + product
        return carry

    lax.fori_loop(0, total, group, 0)


def local(density, centres, exponents, coords, weights, core_density, counts, blocks):
    sources = lax.axis_size("grid")
    columns = lax.axis_size("col")
    rows, cols = density.shape
    points = coords.shape[2]
    f32 = jnp.float32
    params = pltpu.CompilerParams(vmem_limit_bytes=16 * 1024 * 1024)
    table = blocks.T
    shape = jax.ShapeDtypeStruct
    messages = shape((sources, 8, LANES), f32)
    tile_shape = shape((cols // BLK, rows // BLK, BLK, BLK), jnp.bfloat16)
    basis = pltpu.VMEM((rows // BLK + cols // BLK, 4, BLK, LANES), f32)
    listed = shape((sources + 8,), jnp.int32)

    def in_hbm(*arrays):
        return [pltpu.with_memory_space_constraint(array, pltpu.HBM) for array in arrays]

    outgoing, slots = pl.pallas_call(
        pack_kernel,
        out_shape=(shape((sources, 1, 3 * points), f32), shape((columns * NB,), jnp.int32)),
        in_specs=[HBM] * 3,
        out_specs=(VMEM, SMEM),
        scratch_shapes=[
            pltpu.SMEM(table.shape, jnp.int32),
            pltpu.SMEM(counts.shape, jnp.int32),
            pltpu.VMEM((3, NB, points), f32),
            pltpu.SemaphoreType.DMA((3,)),
        ],
        compiler_params=params,
        name="pack",
    )(*in_hbm(table, counts, coords.transpose(1, 0, 2)))
    arrived = lax.all_to_all(outgoing, "grid", split_axis=0, concat_axis=0, tiled=True)
    spacing = exponents.reshape(-1, LANES)
    pieces, forward, backward, scale, work = pl.pallas_call(
        partial(prepare_kernel, group=sources // columns),
        out_shape=(
            shape((rows // BLK + cols // BLK, BLK, BLK), jnp.bfloat16),
            tile_shape,
            tile_shape,
            shape((3, NB * HALVES, LANES), f32),
            listed,
        ),
        in_specs=[HBM] * 7,
        out_specs=(VMEM,) * 4 + (SMEM,),
        scratch_shapes=[
            pltpu.SMEM(table.shape, jnp.int32),
            pltpu.SMEM(counts.shape, jnp.int32),
            pltpu.VMEM(centres.shape, f32),
            pltpu.VMEM(spacing.shape, f32),
            pltpu.VMEM(weights.shape, f32),
            pltpu.VMEM(core_density.shape, f32),
            pltpu.VMEM(density.shape, density.dtype),
            pltpu.VMEM((8 + BLK, LANES), f32),
            pltpu.SemaphoreType.DMA((7,)),
        ],
        compiler_params=params,
        name="prepare",
    )(*in_hbm(table, counts, centres, spacing, weights, core_density, density))
    most = 2 * (sources // GROUP)
    hold = pltpu.VMEM((2, GROUP, 2, BLK, LANES), f32)
    copy_sems = pltpu.SemaphoreType.DMA((2,))
    partials, done, kept = pl.pallas_call(
        density_kernel,
        out_shape=(
            messages,
            shape((most * GROUP + 8,), jnp.int32),
            pltpu.HBM((most, GROUP, 2, BLK, LANES), f32),
        ),
        in_specs=[SMEM] + [VMEM] * 4,
        out_specs=(VMEM, SMEM, HBM),
        scratch_shapes=[pltpu.SMEM((sources + 8,), jnp.int32), basis, hold, copy_sems],
        compiler_params=params,
        name="density",
    )(work, arrived, pieces, forward, backward)
    returned = lax.all_to_all(partials, "grid", split_axis=0, concat_axis=0, tiled=True)
    copies = pl.pallas_call(
        collect_kernel,
        out_shape=shape((columns, NB, 8, LANES), f32),
        in_specs=[SMEM, VMEM],
        out_specs=VMEM,
        compiler_params=params,
        name="collect",
    )(slots, returned)
    everything = lax.all_to_all(copies, "col", split_axis=0, concat_axis=0, tiled=True)
    sending, orbital_charge_samples, xc_batch_amounts = pl.pallas_call(
        point_kernel,
        out_shape=(messages, shape((NB, points), f32), shape((NB,), f32)),
        in_specs=[SMEM, VMEM, VMEM],
        out_specs=(VMEM, VMEM, SMEM),
        scratch_shapes=[
            pltpu.VMEM((NB * 8, LANES), f32),
            pltpu.VMEM((NB * 8, LANES), f32),
            pltpu.VMEM((2, NB * HALVES, LANES), f32),
        ],
        compiler_params=params,
        name="points",
    )(slots, everything, scale)
    factors = lax.all_to_all(sending, "grid", split_axis=0, concat_axis=0, tiled=True)
    potential_matrix_xc = pl.pallas_call(
        potential_kernel,
        out_shape=shape((rows, cols), f32),
        in_specs=[SMEM] + [VMEM] * 3 + [HBM],
        out_specs=VMEM,
        scratch_shapes=[basis, hold, copy_sems],
        compiler_params=params,
        name="potential",
    )(done, arrived, factors, pieces, *in_hbm(kept))
    return (potential_matrix_xc, orbital_charge_samples, xc_batch_amounts)


def solution(mesh):
    return jax.shard_map(
        local,
        mesh=mesh,
        in_specs=(
            P("grid", "col"),
            P(),
            P(),
            P("grid", None, None),
            P("grid", None),
            P("grid", None),
            P("grid"),
            P(),
        ),
        out_specs=(P("grid", "col"), P("grid", None), P("grid")),
        check_vma=False,
    )
```

time: 101 us -> 103 us (1.020)
  Pallas kernels: 22.9 us -> 27.9 us
  local copies, waits for them, and re-layouts: 3.72 us -> 0 us
  waiting for transfers between devices: 4.76 us -> 7.4 us
    unnamed x14 -> x0, local copies, waits for them, and re-layouts: 3.72 us -> none
    all_to_all x1, waiting for transfers between devices: 4.76 us -> 7.4 us  [local(): lax.all_to_all(outgoing, 'grid', split_axis=0, concat_axis=0, tiled=True)]
    pallas_call x1, Pallas kernels: 8.1 us -> 10.6 us  [local(): pl.pallas_call(potential_kernel, out_shape=shape((rows, cols), f32), in_s...]
    pallas_call x2, Pallas kernels: 8.43 us -> 10.8 us  [the longest x1 9.23 us: local(): pl.pallas_call(density_kernel, out_shape=(messages, shape((most * GROUP +...]
    all_to_all x1, blocking collectives: 19.7 us -> 18.6 us  [local(): lax.all_to_all(partials, 'grid', split_axis=0, concat_axis=0, tiled=True)]
  transfers between devices with their start and end apart: 1 -> 1, of which waited for: 1 -> 1; matrix products, arithmetic and copies ran while one was open for 0% -> 0% of each run, Pallas kernels for 5% -> 4%
where the time goes in v5:
time: 103 us
  blocking collectives  52.4 us (51%)
  Pallas kernels  27.9 us (27%)
  starting transfers between devices  14.8 us (14%)
  waiting for transfers between devices  7.4 us (7%)
    all_to_all x1, blocking collectives, local(): lax.all_to_all(sending, 'grid', split_axis=0, concat_axis=0, tiled=True)  19 us
    all_to_all x1, blocking collectives, local(): lax.all_to_all(partials, 'grid', split_axis=0, concat_axis=0, tiled=True)  18.6 us
    all_to_all x1, starting transfers between devices, local(): lax.all_to_all(outgoing, 'grid', split_axis=0, concat_axis=0, tiled=True)  14.8 us
    all_to_all x1, blocking collectives, local(): lax.all_to_all(copies, 'col', split_axis=0, concat_axis=0, tiled=True)  14.7 us
    pallas_call x1, Pallas kernels, local(): pl.pallas_call(potential_kernel, out_shape=shape((rows, cols), f32), in_s...  10.6 us
    pallas_call x1, Pallas kernels, local(): pl.pallas_call(density_kernel, out_shape=(messages, shape((most * GROUP +...  9.23 us
    all_to_all x1, waiting for transfers between devices, local(): lax.all_to_all(outgoing, 'grid', split_axis=0, concat_axis=0, tiled=True)  7.4 us
    pallas_call x1, Pallas kernels, local(): pl.pallas_call(partial(prepare_kernel, group=sources // columns), out_sha...  4.59 us
  transfers between devices with their start and end apart: 1, of which 1 were waited for; matrix products, arithmetic and copies ran while one was open for 0% of the time, Pallas kernels for 4%

profile of v5, /device:TPU:1, one launch (start us, length us, event | category | flops | bytes accessed | tf_op | source)
XLA Modules:
  0.0 103.2 jit_solution(11054140296797873712)
XLA Ops:
  0.6 1.6 %pack.1 = (f32[64,1,768]{2,1,0:T(1,128)}, s32[32]{0:T(128)S(1)}) custom-call(s32[8,256]{1,0:T(8,128)} %bitcast.4, s32[4]{0:T(128)} %counts_hbm.1, f32[3,4,256]{2,1,0:T(4,128)} %bitcast.6), custom_call_target="tpu_custom_call" | custom-call | tf_op jit(solution)/shard_map/pack/pallas_call | solution.py:422
  2.2 14.8 %all-to-all-start = ((f32[64,1,768]{2,1,0:T(1,128)}), f32[64,1,768]{2,1,0:T(1,128)S(1)}, u32[]{:S(2)}, u32[]{:S(2)}) async-start(f32[64,1,768]{2,1,0:T(1,128)} %get-tuple-element.17), calls=%async_computation | async-start | bytes 393216 | tf_op jit(solution)/shard_map/all_to_all | solution.py:436
  17.1 4.6 %prepare.1 = (bf16[18,128,128]{2,1,0:T(8,128)(2,1)S(1)}, bf16[16,2,128,128]{3,2,1,0:T(8,128)(2,1)S(1)}, bf16[16,2,128,128]{3,2,1,0:T(8,128)(2,1)S(1)}, f32[3,8,128]{2,1,0:T(8,128)S(1)}, s32[72]{0:T(128)S(1)}) custom-call(s32[8,256]{1,0:T(8,128)} %bitcast.5, s32[4]{0:T(128)} %counts_hbm.1, f32[3,16384]{1,0:T(4,128)} %refs_2_.1, f32[128,128]{1,0:T(8,128)} %bitcast.3, ...), custom_call_target="tpu_custom_call" | custom-call | tf_op jit(solution)/shard_map/prepare/pallas_call | solution.py:438
  21.7 7.4 %all-to-all-done.arrived = f32[64,1,768]{2,1,0:T(1,128)S(1)} async-done(((f32[64,1,768]{2,1,0:T(1,128)}), f32[64,1,768]{2,1,0:T(1,128)S(1)}, u32[]{:S(2)}, u32[]{:S(2)}) %all-to-all-start) | async-done | bytes 196640 | tf_op jit(solution)/shard_map/all_to_all | solution.py:436
  29.1 9.2 %density.1 = (f32[64,8,128]{2,1,0:T(8,128)S(1)}, s32[136]{0:T(256)S(1)}, f32[32,4,2,128,128]{4,3,2,1,0:T(8,128)}) custom-call(s32[72]{0:T(128)S(1)} %get-tuple-element.16.work, f32[64,1,768]{2,1,0:T(1,128)S(1)} %all-to-all-done.arrived, bf16[18,128,128]{2,1,0:T(8,128)(2,1)S(1)} %get-tuple-element.18.pieces, ...), custom_call_target="tpu_custom_call" | custom-call | tf_op jit(solution)/shard_map/density/pallas_call | solution.py:466
  38.3 18.6 %all_to_all.20.arrived = f32[64,8,128]{2,1,0:T(8,128)S(1)} all-to-all(f32[64,8,128]{2,1,0:T(8,128)S(1)} %get-tuple-element.23), channel_id=1, replica_groups=mesh['grid'=64,'col'=8] {'grid'}, dimensions={0} | all-to-all | bytes 524288 | tf_op jit(solution)/shard_map/all_to_all | solution.py:479
  56.9 0.6 collect.1
  57.5 14.7 %all_to_all.21.sums = f32[8,4,8,128]{3,2,1,0:T(8,128)S(1)} all-to-all(f32[8,4,8,128]{3,2,1,0:T(8,128)S(1)} %collect.1), channel_id=1, replica_groups=mesh['grid'=64,'col'=8] {'col'}, dimensions={0} | all-to-all | bytes 262144 | tf_op jit(solution)/shard_map/all_to_all | solution.py:488
  72.2 1.2 %points.1 = (f32[64,8,128]{2,1,0:T(8,128)S(1)}, f32[4,256]{1,0:T(4,128)}, f32[4]{0:T(128)}) custom-call(s32[32]{0:T(128)S(1)} %get-tuple-element.22.slots, f32[8,4,8,128]{3,2,1,0:T(8,128)S(1)} %all_to_all.21.sums, f32[3,8,128]{2,1,0:T(8,128)S(1)} %get-tuple-element.24.scale), custom_call_target="tpu_custom_call" | custom-call | tf_op jit(solution)/shard_map/points/pallas_call | solution.py:489
  73.5 19.0 %all_to_all.22.factors = f32[64,8,128]{2,1,0:T(8,128)S(1)} all-to-all(f32[64,8,128]{2,1,0:T(8,128)S(1)} %get-tuple-element.25), channel_id=1, replica_groups=mesh['grid'=64,'col'=8] {'grid'}, dimensions={0} | all-to-all | bytes 524288 | tf_op jit(solution)/shard_map/all_to_all | solution.py:502
  92.5 10.6 %potential.1 = f32[256,2048]{1,0:T(8,128)} custom-call(s32[136]{0:T(256)S(1)} %get-tuple-element.21.done, f32[64,1,768]{2,1,0:T(1,128)S(1)} %all-to-all-done.arrived, f32[64,8,128]{2,1,0:T(8,128)S(1)} %all_to_all.22.factors, bf16[18,128,128]{2,1,0:T(8,128)(2,1)S(1)} %get-tuple-element.18.pieces, f32[32,4,2,128,128]{4,3,2,1,0:T(8,128)} %get-tuple-element.26.kept), custom_call_target="tpu_custom_call" | custom-call | tf_op jit(solution)/shard_map/potential/pallas_call | solution.py:503
Async XLA Ops:
  2.2 26.8 %all-to-all-start = ((f32[64,1,768]{2,1,0:T(1,128)}), f32[64,1,768]{2,1,0:T(1,128)S(1)}, u32[]{:S(2)}, u32[]{:S(2)}) async-start(f32[64,1,768]{2,1,0:T(1,128)} %get-tuple-element.17), calls=%async_computation | async-start | bytes 393216 | tf_op jit(solution)/shard_map/all_to_all | solution.py:436

commit v6 on v5

--- a/solution.py
+++ b/solution.py
@@ -25,7 +25,6 @@
 
 PIECES = 3
 GROUP = 4
-REAL = 1 << 16
 FAR = 64.0
 LOG2E = math.log2(math.e)
 SLOPE = 2.0 * math.log(2.0)
@@ -161,7 +160,7 @@
     half = entry & 1
     block = lax.shift_right_logical(entry, 1) & 15
     row = lax.shift_right_logical(entry, 5) & 1
-    source = lax.shift_right_logical(entry, 6) & 1023
+    source = lax.shift_right_logical(entry, 6)
     return source, row, block, half
 
 
@@ -185,12 +184,33 @@
         work[filled + unit] = work[jnp.maximum(filled, 1)]
 
 
-def groups_of(work):
-    return (work[0] + GROUP - 1) // GROUP
+def over_groups(work, handle, carry):
+    filled = work[0]
+
+    def group(step, carry):
+        entries = [
+            (work[GROUP * step + unit + 1], GROUP * step + unit < filled) for unit in range(GROUP)
+        ]
+        return handle(entries, carry)
+
+    return lax.fori_loop(0, (filled + GROUP - 1) // GROUP, group, carry)
+
+
+def over_halves(work, later, arrived, handle):
+    def first_halves(entries, filled):
+        for entry, real in entries:
+            beyond = point_of(arrived, lax.shift_right_logical(entry, 6), 1)[0][0, 0]
+            later[filled + 1] = entry + 1
+            filled = filled + jnp.where(jnp.logical_and(beyond < FAR, real), 1, 0)
+        handle(entries, 0)
+        return filled
+
+    close_list(later, over_groups(work, first_halves, jnp.int32(0)))
+    over_groups(later, handle, 0)
 
 
 def density_kernel(
-    work, arrived, pieces, forward, backward, out, done, kept, later, basis, hold, sems
+    work, arrived, pieces, forward, backward, out, later, basis
 ):
     row_blocks = forward.shape[1]
     spread(pieces, basis)
@@ -218,54 +238,16 @@
         for comp in range(3):
             moment = total_rows(row_slope * row_side(comp) + col_slope * col_side(comp))
             sums.append(SLOPE * (point[comp] * slope - moment))
-        return source, half, sums, row_values, col_values
-
-    def write_back(index):
-        slot = index & 1
-        return pltpu.make_async_copy(hold.at[slot], kept.at[index], sems.at[slot])
-
-    def group(work, step, index):
-        @pl.when(index >= 2)
-        def _():
-            write_back(index - 2).wait()
-
-        entries = [work[GROUP * step + unit + 1] for unit in range(GROUP)]
-        results = [partial_sums(entry) for entry in entries]
-        for unit, (source, half, sums, row_values, col_values) in enumerate(results):
+        return source, half, sums
+
+    def halves(entries, carry):
+        results = [partial_sums(entry) for entry, _ in entries]
+        for source, half, sums in results:
             for comp in range(4):
                 out[source, pl.ds(half * 4 + comp, 1), :] = sums[comp]
-            hold[index & 1, unit, 0] = row_values
-            hold[index & 1, unit, 1] = col_values
-            real = jnp.where(GROUP * step + unit < work[0], REAL, 0)
-            done[GROUP * index + unit + 1] = entries[unit] + real
-        write_back(index).start()
-
-    def first_halves(step, filled):
-        for unit in range(GROUP):
-            entry = work[GROUP * step + unit + 1]
-            beyond = point_of(arrived, decode(entry)[0], 1)[0][0, 0]
-            later[filled + 1] = entry + 1
-            real = jnp.logical_and(beyond < FAR, GROUP * step + unit < work[0])
-            filled = filled + jnp.where(real, 1, 0)
-        group(work, step, step)
-        return filled
-
-    firsts = groups_of(work)
-    filled = lax.fori_loop(0, firsts, first_halves, jnp.int32(0))
-    close_list(later, filled)
-
-    def second_halves(step, carry):
-        group(later, step, firsts + step)
         return carry
 
-    total = firsts + groups_of(later)
-    lax.fori_loop(0, groups_of(later), second_halves, 0)
-    done[0] = total
-    for back in (2, 1):
-
-        @pl.when(total >= back)
-        def _():
-            write_back(total - back).wait()
+    over_halves(work, later, arrived, halves)
 
 
 def collect_kernel(slots, arrived, out):
@@ -335,24 +317,14 @@
         energy_out[batch] = jnp.sum(results_at[1, pl.ds(batch * HALVES, HALVES), :])
 
 
-def potential_kernel(done, arrived, factors, pieces, kept, out, basis, held, sems):
+def potential_kernel(work, arrived, factors, pieces, out, later, basis):
     row_blocks = out.shape[0] // BLK
-    total = done[0]
-
-    def fetch(index):
-        slot = index & 1
-        return pltpu.make_async_copy(kept.at[index], held.at[slot], sems.at[slot])
-
-    @pl.when(total > 0)
-    def _():
-        fetch(0).start()
-
     spread(pieces, basis)
     out[...] = jnp.zeros_like(out)
 
-    def tile_of(entry, row_values, col_values):
+    def tile_of(entry, real):
         source, row, block, half = decode(entry)
-        keep = jnp.where(entry >= REAL, 1.0, 0.0).astype(jnp.float32)
+        keep = jnp.where(real, 1.0, 0.0).astype(jnp.float32)
         point = point_of(arrived, source, half)
         factor = [factors[source, pl.ds(half * 4 + comp, 1), :] * keep for comp in range(4)]
         push = [SLOPE * factor[comp + 1] for comp in range(3)]
@@ -364,6 +336,8 @@
         row_side = side_of(basis, row)
         col_side = side_of(basis, row_blocks + block)
 
+        row_values = values_of(row_side, point)
+        col_values = values_of(col_side, point)
         row_across = row_values * turn(row_side)
         along = col_values * (factor[0] + turn(col_side))
         left_side = jnp.concatenate(
@@ -382,24 +356,14 @@
         col_start = pl.multiple_of(block * BLK, BLK)
         return row_start, col_start, product
 
-    def group(index, carry):
-        @pl.when(index + 1 < total)
-        def _():
-            fetch(index + 1).start()
-
-        fetch(index).wait()
-        results = [
-            tile_of(
-                done[GROUP * index + unit + 1], held[index & 1, unit, 0], held[index & 1, unit, 1]
-            )
-            for unit in range(GROUP)
-        ]
+    def handle(entries, carry):
+        results = [tile_of(entry, real) for entry, real in entries]
         for row_start, col_start, product in results:
             place = (pl.ds(row_start, BLK), pl.ds(col_start, BLK))
             out[place] = out[place] + product
         return carry
 
-    lax.fori_loop(0, total, group, 0)
+    over_halves(work, later, arrived, handle)
 
 
 def local(density, centres, exponents, coords, weights, core_density, counts, blocks):
@@ -415,6 +379,7 @@
     tile_shape = shape((cols // BLK, rows // BLK, BLK, BLK), jnp.bfloat16)
     basis = pltpu.VMEM((rows // BLK + cols // BLK, 4, BLK, LANES), f32)
     listed = shape((sources + 8,), jnp.int32)
+    later = pltpu.SMEM(listed.shape, jnp.int32)
 
     def in_hbm(*arrays):
         return [pltpu.with_memory_space_constraint(array, pltpu.HBM) for array in arrays]
@@ -460,19 +425,12 @@
         compiler_params=params,
         name="prepare",
     )(*in_hbm(table, counts, centres, spacing, weights, core_density, density))
-    most = 2 * (sources // GROUP)
-    hold = pltpu.VMEM((2, GROUP, 2, BLK, LANES), f32)
-    copy_sems = pltpu.SemaphoreType.DMA((2,))
-    partials, done, kept = pl.pallas_call(
+    partials = pl.pallas_call(
         density_kernel,
-        out_shape=(
-            messages,
-            shape((most * GROUP + 8,), jnp.int32),
-            pltpu.HBM((most, GROUP, 2, BLK, LANES), f32),
-        ),
+        out_shape=messages,
         in_specs=[SMEM] + [VMEM] * 4,
-        out_specs=(VMEM, SMEM, HBM),
-        scratch_shapes=[pltpu.SMEM((sources + 8,), jnp.int32), basis, hold, copy_sems],
+        out_specs=VMEM,
+        scratch_shapes=[later, basis],
         compiler_params=params,
         name="density",
     )(work, arrived, pieces, forward, backward)
@@ -503,12 +461,12 @@
     potential_matrix_xc = pl.pallas_call(
         potential_kernel,
         out_shape=shape((rows, cols), f32),
-        in_specs=[SMEM] + [VMEM] * 3 + [HBM],
+        in_specs=[SMEM] + [VMEM] * 3,
         out_specs=VMEM,
-        scratch_shapes=[basis, hold, copy_sems],
+        scratch_shapes=[later, basis],
         compiler_params=params,
         name="potential",
-    )(done, arrived, factors, pieces, *in_hbm(kept))
+    )(work, arrived, factors, pieces)
     return (potential_matrix_xc, orbital_charge_samples, xc_batch_amounts)
 
 

time: 103 us -> 98.4 us (0.955)
  Pallas kernels: 27.9 us -> 24.2 us
    pallas_call x1, Pallas kernels: 9.23 us -> 7.14 us  [local(): pl.pallas_call(density_kernel, out_shape=messages, in_specs=[SMEM] + [VME...]
    pallas_call x1, Pallas kernels: 10.6 us -> 9.1 us  [local(): pl.pallas_call(potential_kernel, out_shape=shape((rows, cols), f32), in_s...]
  transfers between devices with their start and end apart: 1 -> 1, of which waited for: 1 -> 1; matrix products, arithmetic and copies ran while one was open for 0% -> 0% of each run, Pallas kernels for 4% -> 5%
where the time goes in v6:
time: 98.4 us; the launch traced here: 98.6 us
  blocking collectives  51.5 us (52%)
  Pallas kernels  24.2 us (25%)
  starting transfers between devices  14.8 us (15%)
  waiting for transfers between devices  7.4 us (8%)
    all_to_all x1, blocking collectives, local(): lax.all_to_all(sending, 'grid', split_axis=0, concat_axis=0, tiled=True)  19 us
    all_to_all x1, blocking collectives, local(): lax.all_to_all(partials, 'grid', split_axis=0, concat_axis=0, tiled=True)  17.8 us
    all_to_all x1, starting transfers between devices, local(): lax.all_to_all(outgoing, 'grid', split_axis=0, concat_axis=0, tiled=True)  14.8 us
    all_to_all x1, blocking collectives, local(): lax.all_to_all(copies, 'col', split_axis=0, concat_axis=0, tiled=True)  14.7 us
    pallas_call x1, Pallas kernels, local(): pl.pallas_call(potential_kernel, out_shape=shape((rows, cols), f32), in_s...  9.1 us
    all_to_all x1, waiting for transfers between devices, local(): lax.all_to_all(outgoing, 'grid', split_axis=0, concat_axis=0, tiled=True)  7.4 us
    pallas_call x1, Pallas kernels, local(): pl.pallas_call(density_kernel, out_shape=messages, in_specs=[SMEM] + [VME...  7.14 us
    pallas_call x1, Pallas kernels, local(): pl.pallas_call(partial(prepare_kernel, group=sources // columns), out_sha...  4.59 us
  transfers between devices with their start and end apart: 1, of which 1 were waited for; matrix products, arithmetic and copies ran while one was open for 0% of the time, Pallas kernels for 5%

profile of v6, /device:TPU:1, one launch (start us, length us, event | category | flops | bytes accessed | tf_op | source)
XLA Modules:
  0.0 98.6 jit_solution(7212817063598070583)
XLA Ops:
  0.6 1.6 %pack.1 = (f32[64,1,768]{2,1,0:T(1,128)}, s32[32]{0:T(128)S(1)}) custom-call(s32[8,256]{1,0:T(8,128)} %bitcast.4, s32[4]{0:T(128)} %counts_hbm.1, f32[3,4,256]{2,1,0:T(4,128)} %bitcast.6), custom_call_target="tpu_custom_call" | custom-call | tf_op jit(solution)/shard_map/pack/pallas_call | solution.py:387
  2.2 14.8 %all-to-all-start = ((f32[64,1,768]{2,1,0:T(1,128)}), f32[64,1,768]{2,1,0:T(1,128)S(1)}, u32[]{:S(2)}, u32[]{:S(2)}) async-start(f32[64,1,768]{2,1,0:T(1,128)} %get-tuple-element.14), calls=%async_computation | async-start | bytes 393216 | tf_op jit(solution)/shard_map/all_to_all | solution.py:401
  17.1 4.6 %prepare.1 = (bf16[18,128,128]{2,1,0:T(8,128)(2,1)S(1)}, bf16[16,2,128,128]{3,2,1,0:T(8,128)(2,1)S(1)}, bf16[16,2,128,128]{3,2,1,0:T(8,128)(2,1)S(1)}, f32[3,8,128]{2,1,0:T(8,128)S(1)}, s32[72]{0:T(128)S(1)}) custom-call(s32[8,256]{1,0:T(8,128)} %bitcast.5, s32[4]{0:T(128)} %counts_hbm.1, f32[3,16384]{1,0:T(4,128)} %refs_2_.1, f32[128,128]{1,0:T(8,128)} %bitcast.3, ...), custom_call_target="tpu_custom_call" | custom-call | tf_op jit(solution)/shard_map/prepare/pallas_call | solution.py:403
  21.7 7.4 %all-to-all-done.arrived = f32[64,1,768]{2,1,0:T(1,128)S(1)} async-done(((f32[64,1,768]{2,1,0:T(1,128)}), f32[64,1,768]{2,1,0:T(1,128)S(1)}, u32[]{:S(2)}, u32[]{:S(2)}) %all-to-all-start) | async-done | bytes 196640 | tf_op jit(solution)/shard_map/all_to_all | solution.py:401
  29.1 7.1 %density.1 = f32[64,8,128]{2,1,0:T(8,128)S(1)} custom-call(s32[72]{0:T(128)S(1)} %get-tuple-element.13.work, f32[64,1,768]{2,1,0:T(1,128)S(1)} %all-to-all-done.arrived, bf16[18,128,128]{2,1,0:T(8,128)(2,1)S(1)} %get-tuple-element.16.pieces, bf16[16,2,128,128]{3,2,1,0:T(8,128)(2,1)S(1)} %get-tuple-element.17.forward, ...), custom_call_target="tpu_custom_call" | custom-call | tf_op jit(solution)/shard_map/density/pallas_call | solution.py:428
  36.2 17.8 %all_to_all.20.arrived = f32[64,8,128]{2,1,0:T(8,128)S(1)} all-to-all(f32[64,8,128]{2,1,0:T(8,128)S(1)} %density.1), channel_id=1, replica_groups=mesh['grid'=64,'col'=8] {'grid'}, dimensions={0} | all-to-all | bytes 524288 | tf_op jit(solution)/shard_map/all_to_all | solution.py:437
  54.0 0.6 collect.1
  54.6 14.7 %all_to_all.21.sums = f32[8,4,8,128]{3,2,1,0:T(8,128)S(1)} all-to-all(f32[8,4,8,128]{3,2,1,0:T(8,128)S(1)} %collect.1), channel_id=1, replica_groups=mesh['grid'=64,'col'=8] {'col'}, dimensions={0} | all-to-all | bytes 262144 | tf_op jit(solution)/shard_map/all_to_all | solution.py:446
  69.3 1.2 %points.1 = (f32[64,8,128]{2,1,0:T(8,128)S(1)}, f32[4,256]{1,0:T(4,128)}, f32[4]{0:T(128)}) custom-call(s32[32]{0:T(128)S(1)} %get-tuple-element.15.slots, f32[8,4,8,128]{3,2,1,0:T(8,128)S(1)} %all_to_all.21.sums, f32[3,8,128]{2,1,0:T(8,128)S(1)} %get-tuple-element.19.scale), custom_call_target="tpu_custom_call" | custom-call | tf_op jit(solution)/shard_map/points/pallas_call | solution.py:447
  70.5 19.0 %all_to_all.22.factors = f32[64,8,128]{2,1,0:T(8,128)S(1)} all-to-all(f32[64,8,128]{2,1,0:T(8,128)S(1)} %get-tuple-element.20), channel_id=1, replica_groups=mesh['grid'=64,'col'=8] {'grid'}, dimensions={0} | all-to-all | bytes 524288 | tf_op jit(solution)/shard_map/all_to_all | solution.py:460
  89.5 9.1 %potential.1 = f32[256,2048]{1,0:T(8,128)} custom-call(s32[72]{0:T(128)S(1)} %get-tuple-element.13.work, f32[64,1,768]{2,1,0:T(1,128)S(1)} %all-to-all-done.arrived, f32[64,8,128]{2,1,0:T(8,128)S(1)} %all_to_all.22.factors, bf16[18,128,128]{2,1,0:T(8,128)(2,1)S(1)} %get-tuple-element.16.pieces), custom_call_target="tpu_custom_call" | custom-call | tf_op jit(solution)/shard_map/potential/pallas_call | solution.py:461
Async XLA Ops:
  2.2 26.8 %all-to-all-start = ((f32[64,1,768]{2,1,0:T(1,128)}), f32[64,1,768]{2,1,0:T(1,128)S(1)}, u32[]{:S(2)}, u32[]{:S(2)}) async-start(f32[64,1,768]{2,1,0:T(1,128)} %get-tuple-element.14), calls=%async_computation | async-start | bytes 393216 | tf_op jit(solution)/shard_map/all_to_all | solution.py:401

commit v7 on v6

--- a/solution.py
+++ b/solution.py
@@ -26,6 +26,7 @@
 PIECES = 3
 GROUP = 4
 FAR = 64.0
+PARTS = 4
 LOG2E = math.log2(math.e)
 SLOPE = 2.0 * math.log(2.0)
 HBM = pl.BlockSpec(memory_space=pltpu.HBM)
@@ -61,10 +62,10 @@
 
 
 def prepare_kernel(*refs, group):
-    hbm, (pieces, forward, backward, scale, work) = refs[:7], refs[7:12]
-    table, counts, centres, exponents, weights, core, density = refs[12:19]
-    tile, sems = refs[19:]
-    copies = start_all(list(zip(hbm, refs[12:19])), sems)
+    hbm, (pieces, forward, backward, scale, work, upper, lower) = refs[:7], refs[7:14]
+    table, counts, centres, exponents, weights, core, density = refs[14:21]
+    tile, sems = refs[21:]
+    copies = start_all(list(zip(hbm, refs[14:21])), sems)
     rank = lax.axis_index("grid")
     column = lax.axis_index("col")
     own = rank // group
@@ -75,6 +76,7 @@
         copy.wait()
 
     def list_sources(step, filled):
+        every, high, low = filled
         for unit in range(4):
             source = step * 4 + unit
             code = jnp.int32(0)
@@ -83,12 +85,21 @@
                 code = jnp.where(part < 2, 8 + 2 * batch + part, code)
             choice = lax.shift_right_logical(code, 1) & 3
             target = table[column, source * NB + choice] - column * col_blocks
-            work[filled + 1] = source * 64 + (code & 1) * 32 + target * 2
-            filled = filled + lax.shift_right_logical(code, 3)
-        return filled
-
-    filled = lax.fori_loop(0, sources // 4, list_sources, jnp.int32(0))
-    close_list(work, filled)
+            entry = source * 64 + (code & 1) * 32 + target * 2
+            work[every + 1] = entry
+            upper[high + 1] = entry
+            lower[low + 1] = entry
+            found = lax.shift_right_logical(code, 3)
+            every = every + found
+            low = low + (found & code)
+            high = every - low
+        return every, high, low
+
+    zero = jnp.int32(0)
+    every, high, low = lax.fori_loop(0, sources // 4, list_sources, (zero, zero, zero))
+    close_list(work, every)
+    close_list(upper, high)
+    close_list(lower, low)
 
     for copy in copies[4:6]:
         copy.wait()
@@ -317,7 +328,7 @@
         energy_out[batch] = jnp.sum(results_at[1, pl.ds(batch * HALVES, HALVES), :])
 
 
-def potential_kernel(work, arrived, factors, pieces, out, later, basis):
+def potential_kernel(upper, lower, arrived, factors, pieces, result, out, later, basis, sems):
     row_blocks = out.shape[0] // BLK
     spread(pieces, basis)
     out[...] = jnp.zeros_like(out)
@@ -363,7 +374,18 @@
             out[place] = out[place] + product
         return carry
 
-    over_halves(work, later, arrived, handle)
+    height = BLK // PARTS
+    copies = []
+    for row, work in enumerate((upper, lower)):
+        over_halves(work, later, arrived, handle)
+        for part in range(PARTS):
+            place = (pl.ds(row * BLK + part * height, height), slice(None))
+            copies.append(
+                pltpu.make_async_copy(out.at[place], result.at[place], sems.at[row, part])
+            )
+            copies[-1].start()
+    for copy in copies:
+        copy.wait()
 
 
 def local(density, centres, exponents, coords, weights, core_density, counts, blocks):
@@ -400,7 +422,7 @@
     )(*in_hbm(table, counts, coords.transpose(1, 0, 2)))
     arrived = lax.all_to_all(outgoing, "grid", split_axis=0, concat_axis=0, tiled=True)
     spacing = exponents.reshape(-1, LANES)
-    pieces, forward, backward, scale, work = pl.pallas_call(
+    pieces, forward, backward, scale, work, upper, lower = pl.pallas_call(
         partial(prepare_kernel, group=sources // columns),
         out_shape=(
             shape((rows // BLK + cols // BLK, BLK, BLK), jnp.bfloat16),
@@ -408,9 +430,11 @@
             tile_shape,
             shape((3, NB * HALVES, LANES), f32),
             listed,
+            listed,
+            listed,
         ),
         in_specs=[HBM] * 7,
-        out_specs=(VMEM,) * 4 + (SMEM,),
+        out_specs=(VMEM,) * 4 + (SMEM,) * 3,
         scratch_shapes=[
             pltpu.SMEM(table.shape, jnp.int32),
             pltpu.SMEM(counts.shape, jnp.int32),
@@ -461,12 +485,17 @@
     potential_matrix_xc = pl.pallas_call(
         potential_kernel,
         out_shape=shape((rows, cols), f32),
-        in_specs=[SMEM] + [VMEM] * 3,
-        out_specs=VMEM,
-        scratch_shapes=[later, basis],
+        in_specs=[SMEM] * 2 + [VMEM] * 3,
+        out_specs=HBM,
+        scratch_shapes=[
+            pltpu.VMEM((rows, cols), f32),
+            later,
+            basis,
+            pltpu.SemaphoreType.DMA((2, PARTS)),
+        ],
         compiler_params=params,
         name="potential",
-    )(work, arrived, factors, pieces)
+    )(upper, lower, arrived, factors, pieces)
     return (potential_matrix_xc, orbital_charge_samples, xc_batch_amounts)
 
 

time: 98.4 us -> 98.7 us (level)
  no operation moved by 1% of the time
where the time goes in v7:
time: 98.7 us; the launch traced here: 98.8 us
  blocking collectives  51.5 us (52%)
  Pallas kernels  24.6 us (25%)
  starting transfers between devices  14.8 us (15%)
  waiting for transfers between devices  7.23 us (7%)
    all_to_all x1, blocking collectives, local(): lax.all_to_all(sending, 'grid', split_axis=0, concat_axis=0, tiled=True)  19 us
    all_to_all x1, blocking collectives, local(): lax.all_to_all(partials, 'grid', split_axis=0, concat_axis=0, tiled=True)  17.7 us
    all_to_all x1, starting transfers between devices, local(): lax.all_to_all(outgoing, 'grid', split_axis=0, concat_axis=0, tiled=True)  14.8 us
    all_to_all x1, blocking collectives, local(): lax.all_to_all(copies, 'col', split_axis=0, concat_axis=0, tiled=True)  14.7 us
    pallas_call x1, Pallas kernels, local(): pl.pallas_call(potential_kernel, out_shape=shape((rows, cols), f32), in_s...  9.34 us
    all_to_all x1, waiting for transfers between devices, local(): lax.all_to_all(outgoing, 'grid', split_axis=0, concat_axis=0, tiled=True)  7.23 us
    pallas_call x1, Pallas kernels, local(): pl.pallas_call(density_kernel, out_shape=messages, in_specs=[SMEM] + [VME...  7.14 us
    pallas_call x1, Pallas kernels, local(): pl.pallas_call(partial(prepare_kernel, group=sources // columns), out_sha...  4.77 us
  transfers between devices with their start and end apart: 1, of which 1 were waited for; matrix products, arithmetic and copies ran while one was open for 0% of the time, Pallas kernels for 5%

profile of v7, /device:TPU:1, one launch (start us, length us, event | category | flops | bytes accessed | tf_op | source)
XLA Modules:
  0.0 98.8 jit_solution(6094620107617863095)
XLA Ops:
  0.6 1.6 %pack.1 = (f32[64,1,768]{2,1,0:T(1,128)}, s32[32]{0:T(128)S(1)}) custom-call(s32[8,256]{1,0:T(8,128)} %bitcast.4, s32[4]{0:T(128)} %counts_hbm.1, f32[3,4,256]{2,1,0:T(4,128)} %bitcast.6), custom_call_target="tpu_custom_call" | custom-call | tf_op jit(solution)/shard_map/pack/pallas_call | solution.py:409
  2.2 14.8 %all-to-all-start = ((f32[64,1,768]{2,1,0:T(1,128)}), f32[64,1,768]{2,1,0:T(1,128)S(1)}, u32[]{:S(2)}, u32[]{:S(2)}) async-start(f32[64,1,768]{2,1,0:T(1,128)} %get-tuple-element.17), calls=%async_computation | async-start | bytes 393216 | tf_op jit(solution)/shard_map/all_to_all | solution.py:423
  17.1 4.8 %prepare.1 = (bf16[18,128,128]{2,1,0:T(8,128)(2,1)S(1)}, bf16[16,2,128,128]{3,2,1,0:T(8,128)(2,1)S(1)}, bf16[16,2,128,128]{3,2,1,0:T(8,128)(2,1)S(1)}, f32[3,8,1...) custom-call(s32[8,256]{1,0:T(8,128)} %bitcast.5, s32[4]{0:T(128)} %counts_hbm.1, ...), custom_call_target="tpu_custom_call" | custom-call | tf_op jit(solution)/shard_map/prepare/pallas_call | solution.py:425
  21.8 7.2 %all-to-all-done.arrived = f32[64,1,768]{2,1,0:T(1,128)S(1)} async-done(((f32[64,1,768]{2,1,0:T(1,128)}), f32[64,1,768]{2,1,0:T(1,128)S(1)}, u32[]{:S(2)}, u32[]{:S(2)}) %all-to-all-start) | async-done | bytes 196640 | tf_op jit(solution)/shard_map/all_to_all | solution.py:423
  29.1 7.1 %density.1 = f32[64,8,128]{2,1,0:T(8,128)S(1)} custom-call(s32[72]{0:T(128)S(1)} %get-tuple-element.19.work, f32[64,1,768]{2,1,0:T(1,128)S(1)} %all-to-all-done.arrived, bf16[18,128,128]{2,1,0:T(8,128)(2,1)S(1)} %get-tuple-element.20.pieces, bf16[16,2,128,128]{3,2,1,0:T(8,128)(2,1)S(1)} %get-tuple-element.21.forward, ...), custom_call_target="tpu_custom_call" | custom-call | tf_op jit(solution)/shard_map/density/pallas_call | solution.py:452
  36.2 17.7 %all_to_all.20.arrived = f32[64,8,128]{2,1,0:T(8,128)S(1)} all-to-all(f32[64,8,128]{2,1,0:T(8,128)S(1)} %density.1), channel_id=1, replica_groups=mesh['grid'=64,'col'=8] {'grid'}, dimensions={0} | all-to-all | bytes 524288 | tf_op jit(solution)/shard_map/all_to_all | solution.py:461
  53.9 0.6 collect.1
  54.5 14.7 %all_to_all.21.sums = f32[8,4,8,128]{3,2,1,0:T(8,128)S(1)} all-to-all(f32[8,4,8,128]{3,2,1,0:T(8,128)S(1)} %collect.1), channel_id=1, replica_groups=mesh['grid'=64,'col'=8] {'col'}, dimensions={0} | all-to-all | bytes 262144 | tf_op jit(solution)/shard_map/all_to_all | solution.py:470
  69.2 1.2 %points.1 = (f32[64,8,128]{2,1,0:T(8,128)S(1)}, f32[4,256]{1,0:T(4,128)}, f32[4]{0:T(128)}) custom-call(s32[32]{0:T(128)S(1)} %get-tuple-element.18.slots, f32[8,4,8,128]{3,2,1,0:T(8,128)S(1)} %all_to_all.21.sums, f32[3,8,128]{2,1,0:T(8,128)S(1)} %get-tuple-element.23.scale), custom_call_target="tpu_custom_call" | custom-call | tf_op jit(solution)/shard_map/points/pallas_call | solution.py:471
  70.5 19.0 %all_to_all.22.factors = f32[64,8,128]{2,1,0:T(8,128)S(1)} all-to-all(f32[64,8,128]{2,1,0:T(8,128)S(1)} %get-tuple-element.24), channel_id=1, replica_groups=mesh['grid'=64,'col'=8] {'grid'}, dimensions={0} | all-to-all | bytes 524288 | tf_op jit(solution)/shard_map/all_to_all | solution.py:484
  89.5 9.3 %potential.1 = f32[256,2048]{1,0:T(8,128)} custom-call(s32[72]{0:T(128)S(1)} %get-tuple-element.15.upper, s32[72]{0:T(128)S(1)} %get-tuple-element.16.lower, f32[64,1,768]{2,1,0:T(1,128)S(1)} %all-to-all-done.arrived, f32[64,8,128]{2,1,0:T(8,128)S(1)} %all_to_all.22.factors, bf16[18,128,128]{2,1,0:T(8,128)(2,1)S(1)} %get-tuple-element.20.pieces), custom_call_target="tpu_custom_call" | custom-call | tf_op jit(solution)/shard_map/potential/pallas_call | solution.py:485
Async XLA Ops:
  2.2 26.8 %all-to-all-start = ((f32[64,1,768]{2,1,0:T(1,128)}), f32[64,1,768]{2,1,0:T(1,128)S(1)}, u32[]{:S(2)}, u32[]{:S(2)}) async-start(f32[64,1,768]{2,1,0:T(1,128)} %get-tuple-element.17), calls=%async_computation | async-start | bytes 393216 | tf_op jit(solution)/shard_map/all_to_all | solution.py:423

commit v8 on v6

--- a/solution.py
+++ b/solution.py
@@ -41,7 +41,7 @@
     return copies
 
 
-def pack_kernel(table_hbm, counts_hbm, coords_hbm, out, slots, table, counts, coords, sems):
+def pack_kernel(table_hbm, counts_hbm, coords_hbm, out, table, counts, coords, sems):
     copies = start_all([(table_hbm, table), (counts_hbm, counts), (coords_hbm, coords)], sems)
     first = lax.axis_index("grid") * NB
     columns = table.shape[0]
@@ -55,16 +55,14 @@
             [jnp.where(live, coords[comp, pl.ds(batch, 1), :], FAR) for comp in range(3)], axis=1
         )
         for column in range(columns):
-            slot = lax.shift_right_logical(table[column, first + batch], 1)
-            slots[column * NB + batch] = slot
-            out[slot] = message
+            out[lax.shift_right_logical(table[column, first + batch], 1)] = message
 
 
 def prepare_kernel(*refs, group):
-    hbm, (pieces, forward, backward, scale, work) = refs[:7], refs[7:12]
-    table, counts, centres, exponents, weights, core, density = refs[12:19]
-    tile, sems = refs[19:]
-    copies = start_all(list(zip(hbm, refs[12:19])), sems)
+    hbm, (pieces, forward, backward, scale, work, slots) = refs[:7], refs[7:13]
+    table, counts, centres, exponents, weights, core, density = refs[13:20]
+    tile, sems = refs[20:]
+    copies = start_all(list(zip(hbm, refs[13:20])), sems)
     rank = lax.axis_index("grid")
     column = lax.axis_index("col")
     own = rank // group
@@ -73,6 +71,10 @@
     sources = table.shape[1] // NB
     for copy in copies[:2]:
         copy.wait()
+    for batch in range(NB):
+        for position in range(table.shape[0]):
+            owner = lax.shift_right_logical(table[position, rank * NB + batch], 1)
+            slots[position * NB + batch] = owner
 
     def list_sources(step, filled):
         for unit in range(4):
@@ -261,7 +263,7 @@
 
 
 def point_kernel(
-    slots, sums, scale, out, charge_out, energy_out, summed, tiles, results_at
+    slots, sums, scale, out, results_at, summed, tiles
 ):
     columns = slots.shape[0] // NB
     for batch in range(NB):
@@ -309,18 +311,20 @@
             out[slots[column * NB + batch]] = tile
     results_at[0] = valence
     results_at[1] = point_scale * energy
+
+
+def potential_kernel(
+    work, arrived, factors, pieces, results_at, out, charge_out, energy_out, later, basis
+):
+    row_blocks = out.shape[0] // BLK
+    spread(pieces, basis)
+    out[...] = jnp.zeros_like(out)
     for batch in range(NB):
         for half in range(HALVES):
             charge_out[pl.ds(batch, 1), pl.ds(half * LANES, LANES)] = results_at[
                 0, pl.ds(batch * HALVES + half, 1), :
             ]
         energy_out[batch] = jnp.sum(results_at[1, pl.ds(batch * HALVES, HALVES), :])
-
-
-def potential_kernel(work, arrived, factors, pieces, out, later, basis):
-    row_blocks = out.shape[0] // BLK
-    spread(pieces, basis)
-    out[...] = jnp.zeros_like(out)
 
     def tile_of(entry, real):
         source, row, block, half = decode(entry)
@@ -384,11 +388,11 @@
     def in_hbm(*arrays):
         return [pltpu.with_memory_space_constraint(array, pltpu.HBM) for array in arrays]
 
-    outgoing, slots = pl.pallas_call(
+    outgoing = pl.pallas_call(
         pack_kernel,
-        out_shape=(shape((sources, 1, 3 * points), f32), shape((columns * NB,), jnp.int32)),
+        out_shape=shape((sources, 1, 3 * points), f32),
         in_specs=[HBM] * 3,
-        out_specs=(VMEM, SMEM),
+        out_specs=VMEM,
         scratch_shapes=[
             pltpu.SMEM(table.shape, jnp.int32),
             pltpu.SMEM(counts.shape, jnp.int32),
@@ -400,7 +404,7 @@
     )(*in_hbm(table, counts, coords.transpose(1, 0, 2)))
     arrived = lax.all_to_all(outgoing, "grid", split_axis=0, concat_axis=0, tiled=True)
     spacing = exponents.reshape(-1, LANES)
-    pieces, forward, backward, scale, work = pl.pallas_call(
+    pieces, forward, backward, scale, work, slots = pl.pallas_call(
         partial(prepare_kernel, group=sources // columns),
         out_shape=(
             shape((rows // BLK + cols // BLK, BLK, BLK), jnp.bfloat16),
@@ -408,9 +412,10 @@
             tile_shape,
             shape((3, NB * HALVES, LANES), f32),
             listed,
+            shape((columns * NB,), jnp.int32),
         ),
         in_specs=[HBM] * 7,
-        out_specs=(VMEM,) * 4 + (SMEM,),
+        out_specs=(VMEM,) * 4 + (SMEM,) * 2,
         scratch_shapes=[
             pltpu.SMEM(table.shape, jnp.int32),
             pltpu.SMEM(counts.shape, jnp.int32),
@@ -444,29 +449,25 @@
         name="collect",
     )(slots, returned)
     everything = lax.all_to_all(copies, "col", split_axis=0, concat_axis=0, tiled=True)
-    sending, orbital_charge_samples, xc_batch_amounts = pl.pallas_call(
+    sending, results = pl.pallas_call(
         point_kernel,
-        out_shape=(messages, shape((NB, points), f32), shape((NB,), f32)),
+        out_shape=(messages, shape((2, NB * HALVES, LANES), f32)),
         in_specs=[SMEM, VMEM, VMEM],
-        out_specs=(VMEM, VMEM, SMEM),
-        scratch_shapes=[
-            pltpu.VMEM((NB * 8, LANES), f32),
-            pltpu.VMEM((NB * 8, LANES), f32),
-            pltpu.VMEM((2, NB * HALVES, LANES), f32),
-        ],
+        out_specs=(VMEM, VMEM),
+        scratch_shapes=[pltpu.VMEM((NB * 8, LANES), f32), pltpu.VMEM((NB * 8, LANES), f32)],
         compiler_params=params,
         name="points",
     )(slots, everything, scale)
     factors = lax.all_to_all(sending, "grid", split_axis=0, concat_axis=0, tiled=True)
-    potential_matrix_xc = pl.pallas_call(
+    potential_matrix_xc, orbital_charge_samples, xc_batch_amounts = pl.pallas_call(
         potential_kernel,
-        out_shape=shape((rows, cols), f32),
-        in_specs=[SMEM] + [VMEM] * 3,
-        out_specs=VMEM,
+        out_shape=(shape((rows, cols), f32), shape((NB, points), f32), shape((NB,), f32)),
+        in_specs=[SMEM] + [VMEM] * 4,
+        out_specs=(VMEM, VMEM, SMEM),
         scratch_shapes=[later, basis],
         compiler_params=params,
         name="potential",
-    )(work, arrived, factors, pieces)
+    )(work, arrived, factors, pieces, results)
     return (potential_matrix_xc, orbital_charge_samples, xc_batch_amounts)
 
 

time: 98.4 us -> 97.9 us (level)
  Pallas kernels: 24.2 us -> 22.7 us
    pallas_call x3, Pallas kernels: 11.9 us -> 10.8 us  [the longest x1 8.61 us: local(): pl.pallas_call(potential_kernel, out_shape=(shape((rows, cols), f32), sha...]
where the time goes in v8:
time: 97.9 us; the launch traced here: 97.5 us
  blocking collectives  51.9 us (53%)
  Pallas kernels  22.7 us (23%)
  starting transfers between devices  14.8 us (15%)
  waiting for transfers between devices  7.34 us (7%)
    all_to_all x1, blocking collectives, local(): lax.all_to_all(sending, 'grid', split_axis=0, concat_axis=0, tiled=True)  19 us
    all_to_all x1, blocking collectives, local(): lax.all_to_all(partials, 'grid', split_axis=0, concat_axis=0, tiled=True)  18.2 us
    all_to_all x1, starting transfers between devices, local(): lax.all_to_all(outgoing, 'grid', split_axis=0, concat_axis=0, tiled=True)  14.8 us
    all_to_all x1, blocking collectives, local(): lax.all_to_all(copies, 'col', split_axis=0, concat_axis=0, tiled=True)  14.7 us
    pallas_call x1, Pallas kernels, local(): pl.pallas_call(potential_kernel, out_shape=(shape((rows, cols), f32), sha...  8.61 us
    all_to_all x1, waiting for transfers between devices, local(): lax.all_to_all(outgoing, 'grid', split_axis=0, concat_axis=0, tiled=True)  7.34 us
    pallas_call x1, Pallas kernels, local(): pl.pallas_call(density_kernel, out_shape=messages, in_specs=[SMEM] + [VME...  6.67 us
    pallas_call x1, Pallas kernels, local(): pl.pallas_call(partial(prepare_kernel, group=sources // columns), out_sha...  4.65 us
  transfers between devices with their start and end apart: 1, of which 1 were waited for; matrix products, arithmetic and copies ran while one was open for 0% of the time, Pallas kernels for 5%

profile of v8, /device:TPU:1, one launch (start us, length us, event | category | flops | bytes accessed | tf_op | source)
XLA Modules:
  0.0 97.5 jit_solution(6646100611059811316)
XLA Ops:
  0.6 1.6 %pack.1 = f32[64,1,768]{2,1,0:T(1,128)} custom-call(s32[8,256]{1,0:T(8,128)} %bitcast.4, s32[4]{0:T(128)} %counts_hbm.1, f32[3,4,256]{2,1,0:T(4,128)} %bitcast.6), custom_call_target="tpu_custom_call" | custom-call | tf_op jit(solution)/shard_map/pack/pallas_call | solution.py:391
  2.2 14.8 %all-to-all-start = ((f32[64,1,768]{2,1,0:T(1,128)}), f32[64,1,768]{2,1,0:T(1,128)S(1)}, u32[]{:S(2)}, u32[]{:S(2)}) async-start(f32[64,1,768]{2,1,0:T(1,128)} %pack.1), calls=%async_computation | async-start | bytes 393216 | tf_op jit(solution)/shard_map/all_to_all | solution.py:405
  17.0 4.6 %prepare.1 = (bf16[18,128,128]{2,1,0:T(8,128)(2,1)S(1)}, bf16[16,2,128,128]{3,2,1,0:T(8,128)(2,1)S(1)}, bf16[16,2,128,128]{3,2,1,0:T(8,128)(2,1)S(1)}, f32[3,8,1...) custom-call(s32[8,256]{1,0:T(8,128)} %bitcast.5, s32[4]{0:T(128)} %counts_hbm.1, f32[3,16384]{1,0:T(4,128)} %refs_2_.1, ...), custom_call_target="tpu_custom_call" | custom-call | tf_op jit(solution)/shard_map/prepare/pallas_call | solution.py:407
  21.7 7.3 %all-to-all-done.arrived = f32[64,1,768]{2,1,0:T(1,128)S(1)} async-done(((f32[64,1,768]{2,1,0:T(1,128)}), f32[64,1,768]{2,1,0:T(1,128)S(1)}, u32[]{:S(2)}, u32[]{:S(2)}) %all-to-all-start) | async-done | bytes 196640 | tf_op jit(solution)/shard_map/all_to_all | solution.py:405
  29.0 6.7 %density.1 = f32[64,8,128]{2,1,0:T(8,128)S(1)} custom-call(s32[72]{0:T(128)S(1)} %get-tuple-element.11.work, f32[64,1,768]{2,1,0:T(1,128)S(1)} %all-to-all-done.arrived, bf16[18,128,128]{2,1,0:T(8,128)(2,1)S(1)} %get-tuple-element.13.pieces, bf16[16,2,128,128]{3,2,1,0:T(8,128)(2,1)S(1)} %get-tuple-element.14.forward, ...), custom_call_target="tpu_custom_call" | custom-call | tf_op jit(solution)/shard_map/density/pallas_call | solution.py:433
  35.7 18.2 %all_to_all.20.arrived = f32[64,8,128]{2,1,0:T(8,128)S(1)} all-to-all(f32[64,8,128]{2,1,0:T(8,128)S(1)} %density.1), channel_id=1, replica_groups=mesh['grid'=64,'col'=8] {'grid'}, dimensions={0} | all-to-all | bytes 524288 | tf_op jit(solution)/shard_map/all_to_all | solution.py:442
  53.9 0.6 collect.1
  54.5 14.7 %all_to_all.21.sums = f32[8,4,8,128]{3,2,1,0:T(8,128)S(1)} all-to-all(f32[8,4,8,128]{3,2,1,0:T(8,128)S(1)} %collect.1), channel_id=1, replica_groups=mesh['grid'=64,'col'=8] {'col'}, dimensions={0} | all-to-all | bytes 262144 | tf_op jit(solution)/shard_map/all_to_all | solution.py:451
  69.2 0.6 points.1
  69.8 19.0 %all_to_all.22.factors = f32[64,8,128]{2,1,0:T(8,128)S(1)} all-to-all(f32[64,8,128]{2,1,0:T(8,128)S(1)} %get-tuple-element.17), channel_id=1, replica_groups=mesh['grid'=64,'col'=8] {'grid'}, dimensions={0} | all-to-all | bytes 524288 | tf_op jit(solution)/shard_map/all_to_all | solution.py:461
  88.8 8.6 %potential.1 = (f32[256,2048]{1,0:T(8,128)}, f32[4,256]{1,0:T(4,128)}, f32[4]{0:T(128)}) custom-call(s32[72]{0:T(128)S(1)} %get-tuple-element.11.work, f32[64,1,768]{2,1,0:T(1,128)S(1)} %all-to-all-done.arrived, f32[64,8,128]{2,1,0:T(8,128)S(1)} %all_to_all.22.factors, bf16[18,128,128]{2,1,0:T(8,128)(2,1)S(1)} %get-tuple-element.13.pieces, ...), custom_call_target="tpu_custom_call" | custom-call | tf_op jit(solution)/shard_map/potential/pallas_call | solution.py:462
Async XLA Ops:
  2.2 26.8 %all-to-all-start = ((f32[64,1,768]{2,1,0:T(1,128)}), f32[64,1,768]{2,1,0:T(1,128)S(1)}, u32[]{:S(2)}, u32[]{:S(2)}) async-start(f32[64,1,768]{2,1,0:T(1,128)} %pack.1), calls=%async_computation | async-start | bytes 393216 | tf_op jit(solution)/shard_map/all_to_all | solution.py:405
